TPU v7x, 256 devices: a whole 4x4x8 slice. The times are simulated.
256 devices in a mesh: parts: 2 (over x_hi), context: 16 (over z, core), tensor: 8 (over y, x_lo).
Axes of the slice: x: 4 (x_hi: 2, x_lo: 2; x = x_hi * 2 + x_lo), y: 4, z: 8, core: 2. Of those that a mesh axis runs over, the one named last changes fastest.
Arguments:
- queries: bfloat16 [8192, 8192], P(('parts', 'context'), 'tensor'), parts along dimension 0, may hold values from -13 to 13
- keys: bfloat16 [8192, 1024], P(('parts', 'context'), 'tensor'), parts along dimension 0, may hold values from -5.2 to 5.2
- values: bfloat16 [8192, 1024], P(('parts', 'context'), 'tensor'), parts along dimension 0, may hold values from -6 to 6
- out_weight: bfloat16 [8192, 4096], P('tensor'), may hold values from -0.1875 to 0.1875
Outputs:
- mixed: bfloat16 [8192, 4096], P(('parts', 'context'), 'tensor'), parts along dimension 0
There are 2 independent parts, one for each index of `parts`. A program takes and returns all parts, laid end to end along the dimension named above; an argument that names none is the same for every part. Nothing has to cross between parts.
All inputs are finite; a program needn't handle non-finite values.
Results may differ from a plain program's by a relative error of at most 0.015.
Values may be sent and summed in bfloat16 or wider, within the bound.
No kernel may reach another device: no remote copies, remote signals or barrier semaphores. Data moves between devices by JAX's collectives and lax.ppermute only.
A program may use at most 64 MiB of HBM per device.

v0:
```python
import jax
import jax.numpy as jnp
from jax import lax
from jax.experimental import pallas as pl
from jax.experimental.pallas import tpu as pltpu
from jax.sharding import Mesh
from jax.sharding import PartitionSpec as P

HD = 128
LOWEST = -1e30
LOG2E = 1.4426950408889634
SCALE = LOG2E * HD ** (-0.5)
PARTS_CONTEXT = ("parts", "z", "core")
VMEM = pl.BlockSpec(memory_space=pltpu.VMEM)
SMEM = pl.BlockSpec(memory_space=pltpu.SMEM)
LIMIT = 20 * 2**20


def params():
    return pltpu.CompilerParams(vmem_limit_bytes=LIMIT)


def cost(keys, rows, heads):
    return pl.CostEstimate(
        flops=4 * keys * rows * heads * HD,
        bytes_accessed=4 * keys * HD + 4 * heads * rows * HD,
        transcendentals=keys * rows * heads,
    )


def absorb(blocks, state, first=False, diag=False):
    q_ref, top_ref, sum_ref, acc_ref = state
    heads = top_ref.shape[0]
    merge = (lambda parts: parts[0] if len(parts) == 1 else jnp.concatenate(parts, 0))
    keys = merge([b[0] for b in blocks])
    values_t = merge([b[1] for b in blocks]).T
    span = keys.shape[0]
    values_t = jnp.concatenate([values_t, jnp.ones((16, span), jnp.bfloat16)], 0)
    if diag:
        shape = (span, q_ref.shape[2])
        keep = lax.broadcasted_iota(jnp.int32, shape, 0) <= lax.broadcasted_iota(jnp.int32, shape, 1)

    def scores_of(h):
        return jnp.dot(keys, q_ref[h], preferred_element_type=jnp.float32) * SCALE

    ahead = scores_of(0)
    for h in range(heads):
        scores = ahead
        if h + 1 < heads:
            ahead = scores_of(h + 1)
        if diag:
            scores = jnp.where(keep, scores, -jnp.inf)
        top = jnp.max(scores, axis=0, keepdims=True)
        if not first:
            old = top_ref[h]
            top = jnp.maximum(old, top)
            shrink = jnp.exp2(old - top)
        weights = jnp.exp2(scores - top).astype(jnp.bfloat16)
        both = jnp.dot(values_t, weights, preferred_element_type=jnp.float32)
        acc, total = both[:HD], both[HD : HD + 1]
        top_ref[h] = top
        if first:
            sum_ref[h] = total
            acc_ref[h] = acc
        else:
            sum_ref[h] = sum_ref[h] * shrink + total
            acc_ref[h] = acc_ref[h] * shrink + acc


def sds(shape, dtype):
    return jax.ShapeDtypeStruct(shape, dtype)


def open_state(where, queries, others, own):
    rows, width = queries.shape
    heads = width // HD

    def kernel(where_ref, queries_ref, others_ref, own_ref, *state):
        for h in range(heads):
            state[0][h] = queries_ref[:, h * HD : (h + 1) * HD].T
            state[0][heads + h] = others_ref[:, h * HD : (h + 1) * HD].T
        absorb([own_ref], [r.at[:heads] for r in state], first=True, diag=True)
        rest = [r.at[heads:] for r in state]

        @pl.when(where_ref[1] == 0)
        def _():
            absorb([own_ref], rest, first=True)

        @pl.when(where_ref[1] != 0)
        def _():
            rest[1][...] = jnp.full(rest[1].shape, LOWEST, jnp.float32)
            rest[2][...] = jnp.zeros(rest[2].shape, jnp.float32)
            rest[3][...] = jnp.zeros(rest[3].shape, jnp.float32)

    return pl.pallas_call(
        kernel,
        out_shape=(
            sds((2 * heads, HD, rows), jnp.bfloat16),
            sds((2 * heads, 1, rows), jnp.float32),
            sds((2 * heads, 1, rows), jnp.float32),
            sds((2 * heads, HD, rows), jnp.float32),
        ),
        in_specs=[SMEM, VMEM, VMEM, VMEM],
        out_specs=(VMEM,) * 4,
        compiler_params=params(),
        cost_estimate=cost(rows, rows, 2 * heads),
        name="open_state",
    )(where, queries, others, own)


def fold(where, state, ahead, behind, step, parting):
    def kernel(where_ref, ahead_ref, behind_ref, *refs):
        live = refs[:4]
        z = where_ref[0]
        size = where_ref[2]

        @pl.when(z + step >= size)
        def _():
            absorb([ahead_ref, behind_ref], live)

        @pl.when((z + step < size) & (z >= step))
        def _():
            absorb([ahead_ref], live)

        if parting:
            out_ref, stat_ref = refs[-2:]
            heads = live[0].shape[0] // 2
            for h in range(heads):
                total = live[2][heads + h]
                scale = jnp.where(total > 0, 1.0 / jnp.where(total > 0, total, 1.0), 0.0)
                out_ref[h] = (live[3][heads + h] * scale).astype(jnp.bfloat16)
                stat_ref[0, h] = live[1][heads + h]
                stat_ref[1, h] = total

    heads, _, rows = state[0].shape
    extra = (sds((heads // 2, HD, rows), jnp.bfloat16), sds((2, heads // 2, 1, rows), jnp.float32)) if parting else ()
    out = pl.pallas_call(
        kernel,
        out_shape=tuple(sds(a.shape, a.dtype) for a in state) + extra,
        in_specs=[SMEM] + [VMEM] * 6,
        out_specs=(VMEM,) * (4 + len(extra)),
        input_output_aliases={3 + i: i for i in range(4)},
        compiler_params=params(),
        cost_estimate=cost(2 * ahead.shape[1], rows, heads),
    )(where, ahead, behind, *state)
    return (out[:4], out[4:]) if parting else out


def join(where, state, parted, stats, ahead, step):
    heads, _, rows = parted.shape

    def kernel(where_ref, parted_ref, stats_ref, ahead_ref, *refs):
        state_in, state_out = refs[:4], refs[4:]
        live = (state_in[0].at[:heads],) + tuple(state_out)
        for h in range(heads):
            old, theirs = state_in[1][h], stats_ref[0, h]
            top = jnp.maximum(old, theirs)
            mine = jnp.exp2(old - top)
            part = jnp.exp2(theirs - top) * stats_ref[1, h]
            state_out[0][h] = top
            state_out[1][h] = state_in[2][h] * mine + part
            state_out[2][h] = state_in[3][h] * mine + parted_ref[h].astype(jnp.float32) * part

        @pl.when(where_ref[0] >= step)
        def _():
            absorb([ahead_ref], live)

    return pl.pallas_call(
        kernel,
        out_shape=tuple(sds((heads, *a.shape[1:]), a.dtype) for a in state[1:]),
        in_specs=[SMEM] + [VMEM] * 7,
        out_specs=(VMEM,) * 3,
        compiler_params=params(),
        cost_estimate=cost(ahead.shape[1], rows, heads),
        name="join",
    )(where, parted, stats, ahead, *state)


def close(where, state, ahead, step, out_weight, pieces):
    heads, _, rows = state[3].shape
    width = out_weight.shape[1] // pieces

    def kernel(where_ref, ahead_ref, q_ref, top_ref, sum_ref, acc_ref, weight_ref, out_ref, live_top, live_sum, live_acc, att_ref):
        live = (q_ref.at[:heads], live_top, live_sum, live_acc)

        @pl.when(pl.program_id(0) == 0)
        def _():
            for src, dst in zip((top_ref, sum_ref, acc_ref), live[1:]):
                dst[...] = src[...]

            @pl.when(where_ref[0] >= step)
            def _():
                absorb([ahead_ref], live)

            for h in range(heads):
                att_ref[:, h * HD : (h + 1) * HD] = (live_acc[h] / live_sum[h]).T.astype(jnp.bfloat16)

        out_ref[0] = jnp.dot(att_ref[...], weight_ref[...], preferred_element_type=jnp.float32).astype(jnp.bfloat16)

    fixed = lambda a: pl.BlockSpec(a.shape, lambda j, n=a.ndim: (0,) * n)
    return pl.pallas_call(
        kernel,
        grid=(pieces,),
        out_shape=sds((pieces, rows, width), jnp.bfloat16),
        in_specs=[SMEM, fixed(ahead)]
        + [fixed(a) for a in state]
        + [pl.BlockSpec((heads * HD, width), lambda j: (0, j))],
        out_specs=pl.BlockSpec((1, rows, width), lambda j: (j, 0, 0)),
        scratch_shapes=[
            pltpu.VMEM((heads, 1, rows), jnp.float32),
            pltpu.VMEM((heads, 1, rows), jnp.float32),
            pltpu.VMEM((heads, HD, rows), jnp.float32),
            pltpu.VMEM((rows, heads * HD), jnp.bfloat16),
        ],
        compiler_params=params(),
        cost_estimate=cost(2 * rows, rows, heads),
        name="close",
    )(where, ahead, *state, out_weight)


def steps(queries, keys, values, out_weight):
    chips = lax.axis_size("z")
    where = jnp.stack([lax.axis_index("z"), lax.axis_index("core"), jnp.int32(chips)]).astype(jnp.int32)
    up = [(i, (i + 1) % chips) for i in range(chips)]
    down = [(i, (i - 1) % chips) for i in range(chips)]
    swap = lambda a: lax.ppermute(a, "core", [(0, 1), (1, 0)])
    others = swap(queries)
    own = jnp.stack([keys, values])
    half = chips // 2
    ahead, behind = [own], [own]
    for k in range(1, half + 1):
        ahead.append(lax.ppermute(ahead[-1], "z", up))
        if k < half:
            behind.append(lax.ppermute(behind[-1], "z", down))
    state = open_state(where, queries, others, own)
    for k in range(1, half):
        state = fold(where, state, ahead[k], behind[k], k, k + 1 == half)
    state, (parted, stats) = state
    parted, stats = swap(parted), swap(stats)
    last = swap(ahead[half])
    mine = join(where, state, parted, stats, ahead[half], half)
    pieces = lax.axis_size("tensor")
    terms = close(where, (state[0], *mine), last, half, out_weight, pieces)
    got = lax.all_to_all(terms, "tensor", 0, 0, tiled=True)
    return jnp.sum(got.astype(jnp.float32), axis=0).astype(jnp.bfloat16)


def solution(mesh):
    finer = Mesh(
        mesh.devices.reshape(mesh.shape["parts"], mesh.shape["context"] // 2, 2, mesh.shape["tensor"]),
        ("parts", "z", "core", "tensor"),
    )
    in_specs = (
        P(PARTS_CONTEXT, "tensor"),
        P(PARTS_CONTEXT, "tensor"),
        P(PARTS_CONTEXT, "tensor"),
        P("tensor", None),
    )
    out_specs = P(PARTS_CONTEXT, "tensor")
    return jax.shard_map(steps, mesh=finer, in_specs=in_specs, out_specs=out_specs, check_vma=False)
```

profile of v0, /device:TPU:4, one launch (start us, length us, event | category | flops | bytes accessed | tf_op | source)
XLA Modules:
  0.0 82.0 jit_solution(16581145017459715131)
XLA Ops:
  0.0 0.9 %pad_maximum_fusion.own_ref = bf16[2,256,128]{2,1,0:T(8,128)(2,1)S(1)} fusion(bf16[1,256,128]{2,1,0:T(8,128)(2,1)} %bitcast.6, bf16[1,256,128]{2,1,0:T(8,128)(2,1)} %bitcast.7), kind=kLoop, calls=%fused_computation | loop fusion | flops 65536 | bytes 262144 | tf_op jit(solution)/shard_map/stack | solution.py:228
  0.9 2.0 %collective-permute-start = (bf16[2,256,128]{2,1,0:T(8,128)(2,1)S(1)}, bf16[2,256,128]{2,1,0:T(8,128)(2,1)S(1)}, u32[]{:S(2)}, u32[]{:S(2)}) collective-permute-start(bf16[2,256,128]{2,1,0:T(8,128)(2,1)S(1)} %pad_maximum_fusion.own_ref), channel_id=1, source_target_pairs={{0,16},{16,32},{32,48},{48,64},{64,80},{80,96},{96,112},{112,0},{1... | collective-permute-start | bytes 393224 | tf_op jit(solution)/shard_map/ppermute | solution.py:232
  2.9 4.0 %collective-permute-start.5 = (bf16[2,256,128]{2,1,0:T(8,128)(2,1)S(1)}, bf16[2,256,128]{2,1,0:T(8,128)(2,1)S(1)}, u32[]{:S(2)}, u32[]{:S(2)}) collective-permute-start(bf16[2,256,128]{2,1,0:T(8,128)(2,1)S(1)} %pad_maximum_fusion.own_ref), channel_id=1, source_target_pairs={{0,112},{16,0},{32,16},{48,32},{64,48},{80,64},{96,80},{112,96},{1... | collective-permute-start | bytes 393224 | tf_op jit(solution)/shard_map/ppermute | solution.py:234
  6.9 4.1 %collective-permute-done.ahead_ref = bf16[2,256,128]{2,1,0:T(8,128)(2,1)S(1)} collective-permute-done((bf16[2,256,128]{2,1,0:T(8,128)(2,1)S(1)}, bf16[2,256,128]{2,1,0:T(8,128)(2,1)S(1)}, u32[]{:S(2)}, u32[]{:S(2)}) %collective-permute-start) | collective-permute-done | bytes 131104 | tf_op jit(solution)/shard_map/ppermute | solution.py:232
  11.0 3.2 %collective-permute-start.6 = (bf16[2,256,128]{2,1,0:T(8,128)(2,1)S(1)}, bf16[2,256,128]{2,1,0:T(8,128)(2,1)S(1)}, u32[]{:S(2)}, u32[]{:S(2)}) collective-permute-start(bf16[2,256,128]{2,1,0:T(8,128)(2,1)S(1)} %collective-permute-done.5.behind_ref), channel_id=1, source_target_pairs={{0,112},{16,0},{32,16},{48,32},{64,48},{80,64},{96,80},{112,96},{1... | collective-permute-start | bytes 393224 | tf_op jit(solution)/shard_map/ppermute | solution.py:234
  14.2 0.1 pad_add_fusion.where_ref
  14.3 3.2 %collective-permute-done.1.ahead_ref = bf16[2,256,128]{2,1,0:T(8,128)(2,1)S(1)} collective-permute-done((bf16[2,256,128]{2,1,0:T(8,128)(2,1)S(1)}, bf16[2,256,128]{2,1,0:T(8,128)(2,1)S(1)}, u32[]{:S(2)}, u32[]{:S(2)}) %collective-permute-start.1) | collective-permute-done | bytes 131104 | tf_op jit(solution)/shard_map/ppermute | solution.py:232
  17.5 3.2 %collective-permute-start.7 = (bf16[2,256,128]{2,1,0:T(8,128)(2,1)S(1)}, bf16[2,256,128]{2,1,0:T(8,128)(2,1)S(1)}, u32[]{:S(2)}, u32[]{:S(2)}) collective-permute-start(bf16[2,256,128]{2,1,0:T(8,128)(2,1)S(1)} %collective-permute-done.6.behind_ref), channel_id=1, source_target_pairs={{0,112},{16,0},{32,16},{48,32},{64,48},{80,64},{96,80},{112,96},{1... | collective-permute-start | bytes 393224 | tf_op jit(solution)/shard_map/ppermute | solution.py:234
  20.8 1.0 %copy-done = bf16[256,1024]{1,0:T(8,128)(2,1)S(1)} copy-done((bf16[256,1024]{1,0:T(8,128)(2,1)S(1)}, bf16[256,1024]{1,0:T(8,128)(2,1)}, u32[]{:S(2)}) %copy-start) | copy-done | bytes 524312
  21.8 2.9 %open_state.1 = (bf16[16,128,256]{2,1,0:T(8,128)(2,1)S(1)}, f32[16,1,256]{2,1,0:T(1,128)S(1)}, f32[16,1,256]{2,1,0:T(1,128)S(1)}, f32[16,128,256]{2,1,0:T(8,128)S(1)}) custom-call(s32[3]{0:T(128)S(1)} %pad_add_fusion.where_ref, bf16[256,1024]{1,0:T(8,128)(2,1)S(1)} %copy-done, bf16[256,1024]{1,0:T(8,128)(2,1)S(1)} %collective-permute-done.8.others_ref, ...), custom_call_target="tpu_custom_call" | custom-call | flops 536870912 | bytes 2228224 | tf_op jit(solution)/shard_map/open_state/pallas_call | solution.py:95
  24.7 0.0 slice-start
  24.8 0.7 shard_map.46
  25.5 0.0 slice-start.1
  25.5 0.6 shard_map.47
  26.1 0.8 %shard_map.48 = (bf16[16,128,256]{2,1,0:T(8,128)(2,1)S(1)}, f32[16,1,256]{2,1,0:T(1,128)S(1)}, f32[16,1,256]{2,1,0:T(1,128)S(1)}, f32[16,128,256]{2,1,0:T(8,128)...) custom-call(s32[3]{0:T(128)S(1)} %pad_add_fusion.where_ref, ...), custom_call_target="tpu_custom_call", output_to_operand_aliasing={{0}: (3, {}), {1}: (4, {}), {2}: (5, {}), {3}: (6, {})} | custom-call | flops 1073741824 | bytes 2359296 | tf_op jit(solution)/shard_map/pallas_call | solution.py:137
  27.0 0.1 collective-permute-start.9
  27.1 1.2 %collective-permute-start.3 = (bf16[2,256,128]{2,1,0:T(8,128)(2,1)S(1)}, bf16[2,256,128]{2,1,0:T(8,128)(2,1)S(1)}, u32[]{:S(2)}, u32[]{:S(2)}) collective-permute-start(bf16[2,256,128]{2,1,0:T(8,128)(2,1)S(1)} %collective-permute-done.2.ahead_ref), channel_id=1, source_target_pairs={{0,16},{16,32},{32,48},{48,64},{64,80},{80,96},{96,112},{112,0},{1... | collective-permute-start | bytes 393224 | tf_op jit(solution)/shard_map/ppermute | solution.py:232
  28.3 13.2 %collective-permute-done.3.ahead_ref = bf16[2,256,128]{2,1,0:T(8,128)(2,1)S(1)} collective-permute-done((bf16[2,256,128]{2,1,0:T(8,128)(2,1)S(1)}, bf16[2,256,128]{2,1,0:T(8,128)(2,1)S(1)}, u32[]{:S(2)}, u32[]{:S(2)}) %collective-permute-start.3) | collective-permute-done | bytes 131104 | tf_op jit(solution)/shard_map/ppermute | solution.py:232
  41.5 0.5 collective-permute-start.10
  42.0 0.9 %collective-permute-done.10.stats_ref = f32[2,8,1,256]{3,2,1,0:T(1,128)S(1)} collective-permute-done((f32[2,8,1,256]{3,2,1,0:T(1,128)S(1)}, f32[2,8,1,256]{3,2,1,0:T(1,128)S(1)}, u32[]{:S(2)}, u32[]{:S(2)}) %collective-permute-start.10) | collective-permute-done | bytes 16416 | tf_op jit(solution)/shard_map/ppermute | solution.py:226
  42.8 0.7 join.1
  43.6 5.1 %close.1 = bf16[8,256,512]{2,1,0:T(8,128)(2,1)S(1)} custom-call(s32[3]{0:T(128)S(1)} %pad_add_fusion.where_ref, bf16[2,256,128]{2,1,0:T(8,128)(2,1)S(1)} %collective-permute-done.4.ahead_ref, bf16[16,128,256]{2,1,0:T(8,128)(2,1)S(1)} %get-tuple-element.38.refs_0_.q_ref, f32[8,1,256]{2,1,0:T(1,128)S(1)} %get-tuple-element.44.top_ref, ...), custom_call_target="tpu_custom_call" | custom-call | flops 536870912 | bytes 1310720 | tf_op jit(solution)/shard_map/close/pallas_call | solution.py:201
  48.7 32.3 %all_to_all.5 = bf16[8,256,512]{2,1,0:T(8,128)(2,1)S(1)} all-to-all(bf16[8,256,512]{2,1,0:T(8,128)(2,1)S(1)} %close.1), channel_id=1, replica_groups=mesh['parts'=2,'z'=8,'core'=2,'tensor'=8] {'tensor'}, dimensions={0} | all-to-all | bytes 4194304 | tf_op jit(solution)/shard_map/all_to_all | solution.py:244
  81.0 1.0 %reduce_sum.12 = bf16[256,512]{1,0:T(8,128)(2,1)} reduce(bf16[8,256,512]{2,1,0:T(8,128)(2,1)S(1)} %all_to_all.5, bf16[]{:T(256)} %constant.15.clone.1), dimensions={0}, to_apply=%region_0.0 | reduce | flops 917504 | bytes 2359298 | tf_op jit(solution)/shard_map/reduce_sum | solution.py:245
  (15 shorter events, 0.0 us)
Async XLA Ops:
  0.0 20.8 %collective-permute-start.8 = (bf16[256,1024]{1,0:T(8,128)(2,1)}, bf16[256,1024]{1,0:T(8,128)(2,1)S(1)}, u32[]{:S(2)}, u32[]{:S(2)}) collective-permute-start(bf16[256,1024]{1,0:T(8,128)(2,1)} %queries_ref.1), channel_id=1, source_target_pairs={{0,8},{8,0},{1,9},{9,1},{2,10},{10,2},{3,11},{11,3},{4,12},{12,4},... | collective-permute-start | bytes 1572872 | tf_op jit(solution)/shard_map/ppermute | solution.py:226
  0.9 10.1 %collective-permute-start = (bf16[2,256,128]{2,1,0:T(8,128)(2,1)S(1)}, bf16[2,256,128]{2,1,0:T(8,128)(2,1)S(1)}, u32[]{:S(2)}, u32[]{:S(2)}) collective-permute-start(bf16[2,256,128]{2,1,0:T(8,128)(2,1)S(1)} %pad_maximum_fusion.own_ref), channel_id=1, source_target_pairs={{0,16},{16,32},{32,48},{48,64},{64,80},{80,96},{96,112},{112,0},{1... | collective-permute-start | bytes 393224 | tf_op jit(solution)/shard_map/ppermute | solution.py:232
  2.9 8.1 %collective-permute-start.5 = (bf16[2,256,128]{2,1,0:T(8,128)(2,1)S(1)}, bf16[2,256,128]{2,1,0:T(8,128)(2,1)S(1)}, u32[]{:S(2)}, u32[]{:S(2)}) collective-permute-start(bf16[2,256,128]{2,1,0:T(8,128)(2,1)S(1)} %pad_maximum_fusion.own_ref), channel_id=1, source_target_pairs={{0,112},{16,0},{32,16},{48,32},{64,48},{80,64},{96,80},{112,96},{1... | collective-permute-start | bytes 393224 | tf_op jit(solution)/shard_map/ppermute | solution.py:234
  11.0 6.5 %collective-permute-start.1 = (bf16[2,256,128]{2,1,0:T(8,128)(2,1)S(1)}, bf16[2,256,128]{2,1,0:T(8,128)(2,1)S(1)}, u32[]{:S(2)}, u32[]{:S(2)}) collective-permute-start(bf16[2,256,128]{2,1,0:T(8,128)(2,1)S(1)} %collective-permute-done.ahead_ref), channel_id=1, source_target_pairs={{0,16},{16,32},{32,48},{48,64},{64,80},{80,96},{96,112},{112,0},{1... | collective-permute-start | bytes 393224 | tf_op jit(solution)/shard_map/ppermute | solution.py:232
  11.0 6.5 %collective-permute-start.6 = (bf16[2,256,128]{2,1,0:T(8,128)(2,1)S(1)}, bf16[2,256,128]{2,1,0:T(8,128)(2,1)S(1)}, u32[]{:S(2)}, u32[]{:S(2)}) collective-permute-start(bf16[2,256,128]{2,1,0:T(8,128)(2,1)S(1)} %collective-permute-done.5.behind_ref), channel_id=1, source_target_pairs={{0,112},{16,0},{32,16},{48,32},{64,48},{80,64},{96,80},{112,96},{1... | collective-permute-start | bytes 393224 | tf_op jit(solution)/shard_map/ppermute | solution.py:234
  17.5 8.5 %collective-permute-start.2 = (bf16[2,256,128]{2,1,0:T(8,128)(2,1)S(1)}, bf16[2,256,128]{2,1,0:T(8,128)(2,1)S(1)}, u32[]{:S(2)}, u32[]{:S(2)}) collective-permute-start(bf16[2,256,128]{2,1,0:T(8,128)(2,1)S(1)} %collective-permute-done.1.ahead_ref), channel_id=1, source_target_pairs={{0,16},{16,32},{32,48},{48,64},{64,80},{80,96},{96,112},{112,0},{1... | collective-permute-start | bytes 393224 | tf_op jit(solution)/shard_map/ppermute | solution.py:232
  17.5 8.6 %collective-permute-start.7 = (bf16[2,256,128]{2,1,0:T(8,128)(2,1)S(1)}, bf16[2,256,128]{2,1,0:T(8,128)(2,1)S(1)}, u32[]{:S(2)}, u32[]{:S(2)}) collective-permute-start(bf16[2,256,128]{2,1,0:T(8,128)(2,1)S(1)} %collective-permute-done.6.behind_ref), channel_id=1, source_target_pairs={{0,112},{16,0},{32,16},{48,32},{64,48},{80,64},{96,80},{112,96},{1... | collective-permute-start | bytes 393224 | tf_op jit(solution)/shard_map/ppermute | solution.py:234
  20.8 1.0 %copy-start = (bf16[256,1024]{1,0:T(8,128)(2,1)S(1)}, bf16[256,1024]{1,0:T(8,128)(2,1)}, u32[]{:S(2)}) copy-start(bf16[256,1024]{1,0:T(8,128)(2,1)} %queries_ref.1) | copy-start | bytes 1572868
  24.7 18.8 %slice-start = ((s8[8388608]{0:T(1024)(128)(4,1)}), s8[4194304]{0:T(1024)(128)(4,1)S(1)}, s32[]{:S(2)}) async-start(s8[8388608]{0:T(1024)(128)(4,1)} %bitcast.4), calls=%async_computation.1 | async-start | bytes 8388608
  25.5 18.1 %slice-start.1 = ((s8[8388608]{0:T(1024)(128)(4,1)}), s8[4194304]{0:T(1024)(128)(4,1)S(1)}, s32[]{:S(2)}) async-start(s8[8388608]{0:T(1024)(128)(4,1)} %bitcast.4), calls=%async_computation.2 | async-start | bytes 8388608
  27.0 15.9 %collective-permute-start.9 = (bf16[8,128,256]{2,1,0:T(8,128)(2,1)S(1)}, bf16[8,128,256]{2,1,0:T(8,128)(2,1)S(1)}, u32[]{:S(2)}, u32[]{:S(2)}) collective-permute-start(bf16[8,128,256]{2,1,0:T(8,128)(2,1)S(1)} %get-tuple-element.39), channel_id=1, source_target_pairs={{0,8},{8,0},{1,9},{9,1},{2,10},{10,2},{3,11},{11,3},{4,12},{12,4},... | collective-permute-start | bytes 1572872 | tf_op jit(solution)/shard_map/ppermute | solution.py:226
  27.1 14.4 %collective-permute-start.3 = (bf16[2,256,128]{2,1,0:T(8,128)(2,1)S(1)}, bf16[2,256,128]{2,1,0:T(8,128)(2,1)S(1)}, u32[]{:S(2)}, u32[]{:S(2)}) collective-permute-start(bf16[2,256,128]{2,1,0:T(8,128)(2,1)S(1)} %collective-permute-done.2.ahead_ref), channel_id=1, source_target_pairs={{0,16},{16,32},{32,48},{48,64},{64,80},{80,96},{96,112},{112,0},{1... | collective-permute-start | bytes 393224 | tf_op jit(solution)/shard_map/ppermute | solution.py:232
  41.5 2.1 %collective-permute-start.4 = (bf16[2,256,128]{2,1,0:T(8,128)(2,1)S(1)}, bf16[2,256,128]{2,1,0:T(8,128)(2,1)S(1)}, u32[]{:S(2)}, u32[]{:S(2)}) collective-permute-start(bf16[2,256,128]{2,1,0:T(8,128)(2,1)S(1)} %collective-permute-done.3.ahead_ref), channel_id=1, source_target_pairs={{0,8},{8,0},{1,9},{9,1},{2,10},{10,2},{3,11},{11,3},{4,12},{12,4},... | collective-permute-start | bytes 393224 | tf_op jit(solution)/shard_map/ppermute | solution.py:226
  41.5 1.4 %collective-permute-start.10 = (f32[2,8,1,256]{3,2,1,0:T(1,128)S(1)}, f32[2,8,1,256]{3,2,1,0:T(1,128)S(1)}, u32[]{:S(2)}, u32[]{:S(2)}) collective-permute-start(f32[2,8,1,256]{3,2,1,0:T(1,128)S(1)} %get-tuple-element.40), channel_id=1, source_target_pairs={{0,8},{8,0},{1,9},{9,1},{2,10},{10,2},{3,11},{11,3},{4,12},{12,4},... | collective-permute-start | bytes 49160 | tf_op jit(solution)/shard_map/ppermute | solution.py:226
where the time goes:
time: 82.4 us; the launch traced here: 82 us
  blocking collectives  32.3 us (39%)
  waiting for transfers between devices  21.4 us (26%)
  starting transfers between devices  14.3 us (17%)
  Pallas kernels  10.8 us (13%)
  other arithmetic  2.01 us (2%)
  local copies, waits for them, and re-layouts  1.06 us (1%)
    all_to_all x1, blocking collectives, steps(): got = lax.all_to_all(terms, 'tensor', 0, 0, tiled=True)  32.3 us
    ppermute x4, waiting for transfers between devices, steps(): ahead.append(lax.ppermute(ahead[-1], 'z', up))  20.5 us
    ppermute x3, starting transfers between devices, steps(): behind.append(lax.ppermute(behind[-1], 'z', down))  10.5 us
    pallas_call x1, Pallas kernels, close(): pl.pallas_call(kernel, grid=(pieces,), out_shape=sds((pieces, rows, width...  5.06 us
    ppermute x4, starting transfers between devices, steps(): ahead.append(lax.ppermute(ahead[-1], 'z', up))  3.23 us
    pallas_call x1, Pallas kernels, open_state(): pl.pallas_call(kernel, out_shape=(sds((2 * heads, HD, rows), jnp.bfloat16...  2.91 us
    pallas_call x3, Pallas kernels, fold(): pl.pallas_call(kernel, out_shape=tuple((sds(a.shape, a.dtype) for a in st...  2.14 us
  transfers between devices with their start and end apart: 11, of which 4 were waited for; matrix products, arithmetic and copies ran while one was open for 1% of the time, Pallas kernels for 6%

commit v1 on v0

--- a/solution.py
+++ b/solution.py
@@ -7,10 +7,13 @@
 from jax.sharding import PartitionSpec as P
 
 HD = 128
+SIDE = 4
+AWAY = (2, 1, 3)
 LOWEST = -1e30
 LOG2E = 1.4426950408889634
 SCALE = LOG2E * HD ** (-0.5)
 PARTS_CONTEXT = ("parts", "z", "core")
+TENSOR = ("y", "x")
 VMEM = pl.BlockSpec(memory_space=pltpu.VMEM)
 SMEM = pl.BlockSpec(memory_space=pltpu.SMEM)
 LIMIT = 20 * 2**20
@@ -176,51 +179,154 @@
     )(where, parted, stats, ahead, *state)
 
 
-def close(where, state, ahead, step, out_weight, pieces):
+def column(where_ref, step, flip, width):
+    y = lax.rem(where_ref[3] + step, SIDE)
+    x = where_ref[4] if flip == 0 else 1 - where_ref[4]
+    return pl.multiple_of((y * 2 + x) * width, width)
+
+
+def project(att, weight_ref, start, width):
+    return jnp.dot(att, weight_ref[:, pl.ds(start, width)], preferred_element_type=jnp.float32)
+
+
+def close(where, state, ahead, step, out_weight, first, width):
     heads, _, rows = state[3].shape
-    width = out_weight.shape[1] // pieces
-
-    def kernel(where_ref, ahead_ref, q_ref, top_ref, sum_ref, acc_ref, weight_ref, out_ref, live_top, live_sum, live_acc, att_ref):
-        live = (q_ref.at[:heads], live_top, live_sum, live_acc)
-
-        @pl.when(pl.program_id(0) == 0)
-        def _():
-            for src, dst in zip((top_ref, sum_ref, acc_ref), live[1:]):
-                dst[...] = src[...]
-
-            @pl.when(where_ref[0] >= step)
-            def _():
-                absorb([ahead_ref], live)
-
-            for h in range(heads):
-                att_ref[:, h * HD : (h + 1) * HD] = (live_acc[h] / live_sum[h]).T.astype(jnp.bfloat16)
-
-        out_ref[0] = jnp.dot(att_ref[...], weight_ref[...], preferred_element_type=jnp.float32).astype(jnp.bfloat16)
-
-    fixed = lambda a: pl.BlockSpec(a.shape, lambda j, n=a.ndim: (0,) * n)
-    return pl.pallas_call(
-        kernel,
-        grid=(pieces,),
-        out_shape=sds((pieces, rows, width), jnp.bfloat16),
-        in_specs=[SMEM, fixed(ahead)]
-        + [fixed(a) for a in state]
-        + [pl.BlockSpec((heads * HD, width), lambda j: (0, j))],
-        out_specs=pl.BlockSpec((1, rows, width), lambda j: (j, 0, 0)),
-        scratch_shapes=[
-            pltpu.VMEM((heads, 1, rows), jnp.float32),
-            pltpu.VMEM((heads, 1, rows), jnp.float32),
-            pltpu.VMEM((heads, HD, rows), jnp.float32),
-            pltpu.VMEM((rows, heads * HD), jnp.bfloat16),
-        ],
+
+    def kernel(where_ref, ahead_ref, q_ref, top_ref, sum_ref, acc_ref, weight_ref, att_ref, out_ref, *scratch):
+        live = (q_ref.at[:heads], *scratch)
+        for src, dst in zip((top_ref, sum_ref, acc_ref), live[1:]):
+            dst[...] = src[...]
+
+        @pl.when(where_ref[0] >= step)
+        def _():
+            absorb([ahead_ref], live)
+
+        for h in range(heads):
+            att_ref[:, h * HD : (h + 1) * HD] = (live[3][h] / live[2][h]).T.astype(jnp.bfloat16)
+
+        def one(d, _):
+            start = column(where_ref, d, 1, width)
+            out_ref[d] = project(att_ref[:first], weight_ref, start, width).astype(jnp.bfloat16)
+            return 0
+
+        lax.fori_loop(0, SIDE, one, 0)
+
+    return pl.pallas_call(
+        kernel,
+        out_shape=(sds((rows, heads * HD), jnp.bfloat16), sds((SIDE, first, width), jnp.bfloat16)),
+        in_specs=[SMEM] + [VMEM] * 6,
+        out_specs=(VMEM,) * 2,
+        scratch_shapes=[pltpu.VMEM(a.shape, a.dtype) for a in state[1:]],
         compiler_params=params(),
         cost_estimate=cost(2 * rows, rows, heads),
         name="close",
     )(where, ahead, *state, out_weight)
 
 
+def project_away(where, att, out_weight, first, width):
+    rows = att.shape[0] - first
+
+    def kernel(where_ref, att_ref, weight_ref, *outs):
+        for out_ref, d in zip(outs, AWAY):
+            for flip in range(2):
+                terms = project(att_ref[first:], weight_ref, column(where_ref, d, flip, width), width)
+                out_ref[flip] = terms.astype(jnp.bfloat16)
+
+    return pl.pallas_call(
+        kernel,
+        out_shape=(sds((2, rows, width), jnp.bfloat16),) * len(AWAY),
+        in_specs=[SMEM, VMEM, VMEM],
+        out_specs=(VMEM,) * len(AWAY),
+        compiler_params=params(),
+        cost_estimate=cost(2 * rows, rows, 8),
+        name="project_away",
+    )(where, att, out_weight)
+
+
+def project_here(where, att, out_weight, first, width):
+    rows = att.shape[0] - first
+
+    def kernel(where_ref, att_ref, weight_ref, last_ref, first_ref):
+        for flip in range(2):
+            last_ref[flip] = project(att_ref[first:], weight_ref, column(where_ref, 0, flip, width), width)
+
+        def one(d, _):
+            first_ref[d] = project(att_ref[:first], weight_ref, column(where_ref, d, 0, width), width)
+            return 0
+
+        lax.fori_loop(0, SIDE, one, 0)
+
+    return pl.pallas_call(
+        kernel,
+        out_shape=(sds((2, rows, width), jnp.float32), sds((SIDE, first, width), jnp.float32)),
+        in_specs=[SMEM, VMEM, VMEM],
+        out_specs=(VMEM,) * 2,
+        compiler_params=params(),
+        cost_estimate=cost(2 * rows, rows, 8),
+        name="project_here",
+    )(where, att, out_weight)
+
+
+def add_first(kept, got):
+    _, rows, width = kept.shape
+
+    def kernel(kept_ref, got_ref, here_ref, *outs):
+        here_ref[...] = kept_ref[0] + got_ref[0].astype(jnp.float32)
+        for out_ref, d in zip(outs, AWAY):
+            out_ref[...] = (kept_ref[d] + got_ref[d].astype(jnp.float32)).astype(jnp.bfloat16)
+
+    return pl.pallas_call(
+        kernel,
+        out_shape=(sds((rows, width), jnp.float32),) + (sds((rows, width), jnp.bfloat16),) * len(AWAY),
+        in_specs=[VMEM] * 2,
+        out_specs=(VMEM,) * (1 + len(AWAY)),
+        compiler_params=params(),
+        cost_estimate=pl.CostEstimate(flops=kept.size, bytes_accessed=8 * kept.size, transcendentals=0),
+        name="add_first",
+    )(kept, got)
+
+
+def add_last(kept, got):
+    _, rows, width = kept.shape
+
+    def kernel(kept_ref, *refs):
+        *got_refs, here_ref, out_ref = refs
+        here_ref[...] = kept_ref[0] + sum(r[0].astype(jnp.float32) for r in got_refs)
+        out_ref[...] = (kept_ref[1] + sum(r[1].astype(jnp.float32) for r in got_refs)).astype(jnp.bfloat16)
+
+    return pl.pallas_call(
+        kernel,
+        out_shape=(sds((rows, width), jnp.float32), sds((rows, width), jnp.bfloat16)),
+        in_specs=[VMEM] * (1 + len(got)),
+        out_specs=(VMEM,) * 2,
+        compiler_params=params(),
+        cost_estimate=pl.CostEstimate(flops=kept.size, bytes_accessed=8 * kept.size, transcendentals=0),
+        name="add_last",
+    )(kept, *got)
+
+
+def finish(first_here, first_got, last_here, last_got):
+    rows, width = first_here.shape
+    more = last_here.shape[0]
+
+    def kernel(first_ref, *refs):
+        *got_refs, last_ref, swapped_ref, out_ref = refs
+        out_ref[:rows] = (first_ref[...] + sum(r[...].astype(jnp.float32) for r in got_refs)).astype(jnp.bfloat16)
+        out_ref[rows:] = (last_ref[...] + swapped_ref[...].astype(jnp.float32)).astype(jnp.bfloat16)
+
+    return pl.pallas_call(
+        kernel,
+        out_shape=sds((rows + more, width), jnp.bfloat16),
+        in_specs=[VMEM] * (3 + len(first_got)),
+        out_specs=VMEM,
+        compiler_params=params(),
+        name="finish",
+    )(first_here, *first_got, last_here, last_got)
+
+
 def steps(queries, keys, values, out_weight):
     chips = lax.axis_size("z")
-    where = jnp.stack([lax.axis_index("z"), lax.axis_index("core"), jnp.int32(chips)]).astype(jnp.int32)
+    where = jnp.stack([lax.axis_index("z"), lax.axis_index("core"), jnp.int32(chips), lax.axis_index("y"), lax.axis_index("x")]).astype(jnp.int32)
     up = [(i, (i + 1) % chips) for i in range(chips)]
     down = [(i, (i - 1) % chips) for i in range(chips)]
     swap = lambda a: lax.ppermute(a, "core", [(0, 1), (1, 0)])
@@ -239,22 +345,32 @@
     parted, stats = swap(parted), swap(stats)
     last = swap(ahead[half])
     mine = join(where, state, parted, stats, ahead[half], half)
-    pieces = lax.axis_size("tensor")
-    terms = close(where, (state[0], *mine), last, half, out_weight, pieces)
-    got = lax.all_to_all(terms, "tensor", 0, 0, tiled=True)
-    return jnp.sum(got.astype(jnp.float32), axis=0).astype(jnp.bfloat16)
+    width = out_weight.shape[1] // (2 * SIDE)
+    first = queries.shape[0] // 2
+    att, send = close(where, (state[0], *mine), last, half, out_weight, first, width)
+    across = lambda a: lax.ppermute(a, "x", [(0, 1), (1, 0)])
+    along = lambda a, d: lax.ppermute(a, "y", [(i, (i + d) % SIDE) for i in range(SIDE)])
+    got_x = across(send)
+    away = project_away(where, att, out_weight, first, width)
+    got_y = [along(a, d) for a, d in zip(away, AWAY)]
+    last_kept, first_kept = project_here(where, att, out_weight, first, width)
+    first_here, *first_away = add_first(first_kept, got_x)
+    first_got = [along(a, d) for a, d in zip(first_away, AWAY)]
+    last_here, last_away = add_last(last_kept, got_y)
+    last_got = across(last_away)
+    return finish(first_here, first_got, last_here, last_got)
 
 
 def solution(mesh):
     finer = Mesh(
-        mesh.devices.reshape(mesh.shape["parts"], mesh.shape["context"] // 2, 2, mesh.shape["tensor"]),
-        ("parts", "z", "core", "tensor"),
+        mesh.devices.reshape(mesh.shape["parts"], mesh.shape["context"] // 2, 2, SIDE, mesh.shape["tensor"] // SIDE),
+        ("parts", "z", "core", "y", "x"),
     )
     in_specs = (
-        P(PARTS_CONTEXT, "tensor"),
-        P(PARTS_CONTEXT, "tensor"),
-        P(PARTS_CONTEXT, "tensor"),
-        P("tensor", None),
+        P(PARTS_CONTEXT, TENSOR),
+        P(PARTS_CONTEXT, TENSOR),
+        P(PARTS_CONTEXT, TENSOR),
+        P(TENSOR, None),
     )
-    out_specs = P(PARTS_CONTEXT, "tensor")
+    out_specs = P(PARTS_CONTEXT, TENSOR)
     return jax.shard_map(steps, mesh=finer, in_specs=in_specs, out_specs=out_specs, check_vma=False)

time: 82.4 us -> 76 us (0.922)
  blocking collectives: 32.3 us -> 0 us
  starting transfers between devices: 14.3 us -> 28.4 us
  waiting for transfers between devices: 21.4 us -> 32.6 us
  Pallas kernels: 10.8 us -> 12.7 us
  other arithmetic: 2.01 us -> 0.89 us
    all_to_all x1 -> x0, blocking collectives: 32.3 us -> none  [steps(): got = lax.all_to_all(terms, 'tensor', 0, 0, tiled=True)]
    ppermute x0 -> x8, starting transfers between devices: none -> 14.1 us  [the longest x6 11.9 us: steps(): lax.ppermute(a, 'y', [(i, (i + d) % SIDE) for i in range(SIDE)])]
    ppermute x0 -> x8, waiting for transfers between devices: none -> 11.2 us  [the longest x6 11.2 us: steps(): lax.ppermute(a, 'y', [(i, (i + d) % SIDE) for i in range(SIDE)])]
    pallas_call x1 -> x6, Pallas kernels: 5.06 us -> 6.95 us  [the longest x1 2.29 us: project_here(): pl.pallas_call(kernel, out_shape=(sds((2, rows, width), jnp.float32), sds...]
    reduce_sum x1 -> x0, other arithmetic: 1.05 us -> none  [steps(): return jnp.sum(got.astype(jnp.float32), axis=0).astype(jnp.bfloat16)]
  transfers between devices with their start and end apart: 11 -> 19, of which waited for: 4 -> 10; matrix products, arithmetic and copies ran while one was open for 1% -> 1% of each run, Pallas kernels for 6% -> 12%
where the time goes in v1:
time: 76 us; the launch traced here: 75.9 us
  waiting for transfers between devices  32.6 us (43%)
  starting transfers between devices  28.4 us (37%)
  Pallas kernels  12.7 us (17%)
  local copies, waits for them, and re-layouts  1.14 us (1%)
  other arithmetic  0.89 us (1%)
    ppermute x4, waiting for transfers between devices, steps(): ahead.append(lax.ppermute(ahead[-1], 'z', up))  20.5 us
    ppermute x6, starting transfers between devices, steps(): lax.ppermute(a, 'y', [(i, (i + d) % SIDE) for i in range(SIDE)])  11.9 us
    ppermute x6, waiting for transfers between devices, steps(): lax.ppermute(a, 'y', [(i, (i + d) % SIDE) for i in range(SIDE)])  11.2 us
    ppermute x3, starting transfers between devices, steps(): behind.append(lax.ppermute(behind[-1], 'z', down))  10.5 us
    ppermute x4, starting transfers between devices, steps(): ahead.append(lax.ppermute(ahead[-1], 'z', up))  3.23 us
    pallas_call x1, Pallas kernels, open_state(): pl.pallas_call(kernel, out_shape=(sds((2 * heads, HD, rows), jnp.bfloat16...  2.92 us
    pallas_call x1, Pallas kernels, project_here(): pl.pallas_call(kernel, out_shape=(sds((2, rows, width), jnp.float32), sds...  2.29 us
    ppermute x2, starting transfers between devices, steps(): across = lambda a: lax.ppermute(a, 'x', [(0, 1), (1, 0)])  2.2 us
  transfers between devices with their start and end apart: 19, of which 10 were waited for; matrix products, arithmetic and copies ran while one was open for 1% of the time, Pallas kernels for 12%

profile of v1, /device:TPU:4, one launch (start us, length us, event | category | flops | bytes accessed | tf_op | source)
XLA Modules:
  0.0 75.9 jit_solution(10798196045789568650)
XLA Ops:
  0.9 2.0 %collective-permute-start = (bf16[2,256,128]{2,1,0:T(8,128)(2,1)S(1)}, bf16[2,256,128]{2,1,0:T(8,128)(2,1)S(1)}, u32[]{:S(2)}, u32[]{:S(2)}) collective-permute-start(bf16[2,256,128]{2,1,0:T(8,128)(2,1)S(1)} %pad_maximum_fusion.own_ref), channel_id=1, source_target_pairs={{0,16},{16,32},{32,48},{48,64},{64,80},{80,96},{96,112},{112,0},{1... | collective-permute-start | bytes 393224 | tf_op jit(solution)/shard_map/ppermute | solution.py:338
  2.9 4.0 %collective-permute-start.5 = (bf16[2,256,128]{2,1,0:T(8,128)(2,1)S(1)}, bf16[2,256,128]{2,1,0:T(8,128)(2,1)S(1)}, u32[]{:S(2)}, u32[]{:S(2)}) collective-permute-start(bf16[2,256,128]{2,1,0:T(8,128)(2,1)S(1)} %pad_maximum_fusion.own_ref), channel_id=1, source_target_pairs={{0,112},{16,0},{32,16},{48,32},{64,48},{80,64},{96,80},{112,96},{1... | collective-permute-start | bytes 393224 | tf_op jit(solution)/shard_map/ppermute | solution.py:340
  6.9 4.1 %collective-permute-done.ahead_ref = bf16[2,256,128]{2,1,0:T(8,128)(2,1)S(1)} collective-permute-done((bf16[2,256,128]{2,1,0:T(8,128)(2,1)S(1)}, bf16[2,256,128]{2,1,0:T(8,128)(2,1)S(1)}, u32[]{:S(2)}, u32[]{:S(2)}) %collective-permute-start) | collective-permute-done | bytes 131104 | tf_op jit(solution)/shard_map/ppermute | solution.py:338
  11.0 3.2 %collective-permute-start.6 = (bf16[2,256,128]{2,1,0:T(8,128)(2,1)S(1)}, bf16[2,256,128]{2,1,0:T(8,128)(2,1)S(1)}, u32[]{:S(2)}, u32[]{:S(2)}) collective-permute-start(bf16[2,256,128]{2,1,0:T(8,128)(2,1)S(1)} %collective-permute-done.5.behind_ref), channel_id=1, source_target_pairs={{0,112},{16,0},{32,16},{48,32},{64,48},{80,64},{96,80},{112,96},{1... | collective-permute-start | bytes 393224 | tf_op jit(solution)/shard_map/ppermute | solution.py:340
  14.3 3.2 %collective-permute-done.1.ahead_ref = bf16[2,256,128]{2,1,0:T(8,128)(2,1)S(1)} collective-permute-done((bf16[2,256,128]{2,1,0:T(8,128)(2,1)S(1)}, bf16[2,256,128]{2,1,0:T(8,128)(2,1)S(1)}, u32[]{:S(2)}, u32[]{:S(2)}) %collective-permute-start.1) | collective-permute-done | bytes 131104 | tf_op jit(solution)/shard_map/ppermute | solution.py:338
  17.5 3.2 %collective-permute-start.7 = (bf16[2,256,128]{2,1,0:T(8,128)(2,1)S(1)}, bf16[2,256,128]{2,1,0:T(8,128)(2,1)S(1)}, u32[]{:S(2)}, u32[]{:S(2)}) collective-permute-start(bf16[2,256,128]{2,1,0:T(8,128)(2,1)S(1)} %collective-permute-done.6.behind_ref), channel_id=1, source_target_pairs={{0,112},{16,0},{32,16},{48,32},{64,48},{80,64},{96,80},{112,96},{1... | collective-permute-start | bytes 393224 | tf_op jit(solution)/shard_map/ppermute | solution.py:340
  20.8 1.0 %copy-done = bf16[256,1024]{1,0:T(8,128)(2,1)S(1)} copy-done((bf16[256,1024]{1,0:T(8,128)(2,1)S(1)}, bf16[256,1024]{1,0:T(8,128)(2,1)}, u32[]{:S(2)}) %copy-start) | copy-done | bytes 524312
  21.8 2.9 %open_state.1 = (bf16[16,128,256]{2,1,0:T(8,128)(2,1)S(1)}, f32[16,1,256]{2,1,0:T(1,128)S(1)}, f32[16,1,256]{2,1,0:T(1,128)S(1)}, f32[16,128,256]{2,1,0:T(8,128)S(1)}) custom-call(s32[5]{0:T(128)S(1)} %stack.28.where_ref, bf16[256,1024]{1,0:T(8,128)(2,1)S(1)} %copy-done, bf16[256,1024]{1,0:T(8,128)(2,1)S(1)} %collective-permute-done.8.others_ref, ...), custom_call_target="tpu_custom_call" | custom-call | flops 536870912 | bytes 2228224 | tf_op jit(solution)/shard_map/open_state/pallas_call | solution.py:98
  27.1 1.2 %collective-permute-start.3 = (bf16[2,256,128]{2,1,0:T(8,128)(2,1)S(1)}, bf16[2,256,128]{2,1,0:T(8,128)(2,1)S(1)}, u32[]{:S(2)}, u32[]{:S(2)}) collective-permute-start(bf16[2,256,128]{2,1,0:T(8,128)(2,1)S(1)} %collective-permute-done.2.ahead_ref), channel_id=1, source_target_pairs={{0,16},{16,32},{32,48},{48,64},{64,80},{80,96},{96,112},{112,0},{1... | collective-permute-start | bytes 393224 | tf_op jit(solution)/shard_map/ppermute | solution.py:338
  28.3 13.2 %collective-permute-done.3.ahead_ref = bf16[2,256,128]{2,1,0:T(8,128)(2,1)S(1)} collective-permute-done((bf16[2,256,128]{2,1,0:T(8,128)(2,1)S(1)}, bf16[2,256,128]{2,1,0:T(8,128)(2,1)S(1)}, u32[]{:S(2)}, u32[]{:S(2)}) %collective-permute-start.3) | collective-permute-done | bytes 131104 | tf_op jit(solution)/shard_map/ppermute | solution.py:338
  43.6 2.1 %close.1 = (bf16[256,1024]{1,0:T(8,128)(2,1)S(1)}, bf16[4,128,512]{2,1,0:T(8,128)(2,1)S(1)}) custom-call(s32[5]{0:T(128)S(1)} %stack.28.where_ref, bf16[2,256,128]{2,1,0:T(8,128)(2,1)S(1)} %collective-permute-done.4.ahead_ref, bf16[16,128,256]{2,1,0:T(8,128)(2,1)S(1)} %get-tuple-element.51.refs_0_.q_ref, f32[8,1,256]{2,1,0:T(1,128)S(1)} %get-tuple-element.57.top_ref, ...), custom_call_target="tpu_custom_call" | custom-call | flops 536870912 | bytes 1310720 | tf_op jit(solution)/shard_map/close/pallas_call | solution.py:214
  45.7 1.3 %collective-permute-start.11 = (bf16[4,128,512]{2,1,0:T(8,128)(2,1)S(1)}, bf16[4,128,512]{2,1,0:T(8,128)(2,1)S(1)}, u32[]{:S(2)}, u32[]{:S(2)}) collective-permute-start(bf16[4,128,512]{2,1,0:T(8,128)(2,1)S(1)} %get-tuple-element.62), channel_id=1, source_target_pairs={{0,1},{1,0},{2,3},{3,2},{4,5},{5,4},{6,7},{7,6},{8,9},{9,8},{10,11... | collective-permute-start | bytes 1572872 | tf_op jit(solution)/shard_map/ppermute | solution.py:351
  47.0 1.6 %project_away.1 = (bf16[2,128,512]{2,1,0:T(8,128)(2,1)S(1)}, bf16[2,128,512]{2,1,0:T(8,128)(2,1)S(1)}, bf16[2,128,512]{2,1,0:T(8,128)(2,1)S(1)}) custom-call(s32[5]{0:T(128)S(1)} %stack.28.where_ref, bf16[256,1024]{1,0:T(8,128)(2,1)S(1)} %get-tuple-element.60.att_ref, bf16[1024,4096]{1,0:T(8,128)(2,1)S(1)} %bitcast.7), custom_call_target="tpu_custom_call" | custom-call | flops 134217728 | bytes 655360 | tf_op jit(solution)/shard_map/project_away/pallas_call | solution.py:235
  48.6 3.3 %collective-permute-start.15 = (bf16[2,128,512]{2,1,0:T(8,128)(2,1)S(1)}, bf16[2,128,512]{2,1,0:T(8,128)(2,1)S(1)}, u32[]{:S(2)}, u32[]{:S(2)}) collective-permute-start(bf16[2,128,512]{2,1,0:T(8,128)(2,1)S(1)} %get-tuple-element.68), channel_id=1, source_target_pairs={{0,4},{2,6},{4,0},{6,2},{1,5},{3,7},{5,1},{7,3},{8,12},{10,14},{12... | collective-permute-start | bytes 786440 | tf_op jit(solution)/shard_map/ppermute | solution.py:352
  52.6 2.6 %collective-permute-start.17 = (bf16[2,128,512]{2,1,0:T(8,128)(2,1)S(1)}, bf16[2,128,512]{2,1,0:T(8,128)(2,1)S(1)}, u32[]{:S(2)}, u32[]{:S(2)}) collective-permute-start(bf16[2,128,512]{2,1,0:T(8,128)(2,1)S(1)} %get-tuple-element.70), channel_id=1, source_target_pairs={{0,6},{2,0},{4,2},{6,4},{1,7},{3,1},{5,3},{7,5},{8,14},{10,8},{12,... | collective-permute-start | bytes 786440 | tf_op jit(solution)/shard_map/ppermute | solution.py:352
  55.1 2.3 %project_here.1 = (f32[2,128,512]{2,1,0:T(8,128)S(1)}, f32[4,128,512]{2,1,0:T(8,128)S(1)}) custom-call(s32[5]{0:T(128)S(1)} %stack.28.where_ref, bf16[256,1024]{1,0:T(8,128)(2,1)S(1)} %get-tuple-element.60.att_ref, bf16[1024,4096]{1,0:T(8,128)(2,1)S(1)} %bitcast.7), custom_call_target="tpu_custom_call" | custom-call | flops 134217728 | bytes 655360 | tf_op jit(solution)/shard_map/project_here/pallas_call | solution.py:259
  57.4 2.0 %collective-permute-done.15.refs_0_ = bf16[2,128,512]{2,1,0:T(8,128)(2,1)S(1)} collective-permute-done((bf16[2,128,512]{2,1,0:T(8,128)(2,1)S(1)}, bf16[2,128,512]{2,1,0:T(8,128)(2,1)S(1)}, u32[]{:S(2)}, u32[]{:S(2)}) %collective-permute-start.15) | collective-permute-done | bytes 262176 | tf_op jit(solution)/shard_map/ppermute | solution.py:352
  59.4 4.7 %collective-permute-done.16.refs_1_ = bf16[2,128,512]{2,1,0:T(8,128)(2,1)S(1)} collective-permute-done((bf16[2,128,512]{2,1,0:T(8,128)(2,1)S(1)}, bf16[2,128,512]{2,1,0:T(8,128)(2,1)S(1)}, u32[]{:S(2)}, u32[]{:S(2)}) %collective-permute-start.16) | collective-permute-done | bytes 262176 | tf_op jit(solution)/shard_map/ppermute | solution.py:352
  64.6 0.9 %collective-permute-start.18 = (bf16[128,512]{1,0:T(8,128)(2,1)S(1)}, bf16[128,512]{1,0:T(8,128)(2,1)S(1)}, u32[]{:S(2)}, u32[]{:S(2)}) collective-permute-start(bf16[128,512]{1,0:T(8,128)(2,1)S(1)} %get-tuple-element.72), channel_id=1, source_target_pairs={{0,1},{1,0},{2,3},{3,2},{4,5},{5,4},{6,7},{7,6},{8,9},{9,8},{10,11... | collective-permute-start | bytes 393224 | tf_op jit(solution)/shard_map/ppermute | solution.py:351
  65.6 2.1 %collective-permute-start.12 = (bf16[128,512]{1,0:T(8,128)(2,1)S(1)}, bf16[128,512]{1,0:T(8,128)(2,1)S(1)}, u32[]{:S(2)}, u32[]{:S(2)}) collective-permute-start(bf16[128,512]{1,0:T(8,128)(2,1)S(1)} %get-tuple-element.64), channel_id=1, source_target_pairs={{0,4},{2,6},{4,0},{6,2},{1,5},{3,7},{5,1},{7,3},{8,12},{10,14},{12... | collective-permute-start | bytes 393224 | tf_op jit(solution)/shard_map/ppermute | solution.py:352
  67.7 1.5 %collective-permute-start.13 = (bf16[128,512]{1,0:T(8,128)(2,1)S(1)}, bf16[128,512]{1,0:T(8,128)(2,1)S(1)}, u32[]{:S(2)}, u32[]{:S(2)}) collective-permute-start(bf16[128,512]{1,0:T(8,128)(2,1)S(1)} %get-tuple-element.65), channel_id=1, source_target_pairs={{0,2},{2,4},{4,6},{6,0},{1,3},{3,5},{5,7},{7,1},{8,10},{10,12},{12... | collective-permute-start | bytes 393224 | tf_op jit(solution)/shard_map/ppermute | solution.py:352
  69.2 1.8 %collective-permute-start.14 = (bf16[128,512]{1,0:T(8,128)(2,1)S(1)}, bf16[128,512]{1,0:T(8,128)(2,1)S(1)}, u32[]{:S(2)}, u32[]{:S(2)}) collective-permute-start(bf16[128,512]{1,0:T(8,128)(2,1)S(1)} %get-tuple-element.66), channel_id=1, source_target_pairs={{0,6},{2,0},{4,2},{6,4},{1,7},{3,1},{5,3},{7,5},{8,14},{10,8},{12,... | collective-permute-start | bytes 393224 | tf_op jit(solution)/shard_map/ppermute | solution.py:352
  70.9 2.3 %collective-permute-done.12.refs_0_ = bf16[128,512]{1,0:T(8,128)(2,1)S(1)} collective-permute-done((bf16[128,512]{1,0:T(8,128)(2,1)S(1)}, bf16[128,512]{1,0:T(8,128)(2,1)S(1)}, u32[]{:S(2)}, u32[]{:S(2)}) %collective-permute-start.12) | collective-permute-done | bytes 131104 | tf_op jit(solution)/shard_map/ppermute | solution.py:352
  73.3 1.5 %collective-permute-done.13.refs_1_ = bf16[128,512]{1,0:T(8,128)(2,1)S(1)} collective-permute-done((bf16[128,512]{1,0:T(8,128)(2,1)S(1)}, bf16[128,512]{1,0:T(8,128)(2,1)S(1)}, u32[]{:S(2)}, u32[]{:S(2)}) %collective-permute-start.13) | collective-permute-done | bytes 131104 | tf_op jit(solution)/shard_map/ppermute | solution.py:352
  (34 shorter events, 7.7 us)
Async XLA Ops:
  0.0 20.8 %collective-permute-start.8 = (bf16[256,1024]{1,0:T(8,128)(2,1)}, bf16[256,1024]{1,0:T(8,128)(2,1)S(1)}, u32[]{:S(2)}, u32[]{:S(2)}) collective-permute-start(bf16[256,1024]{1,0:T(8,128)(2,1)} %queries_ref.1), channel_id=1, source_target_pairs={{0,8},{8,0},{1,9},{9,1},{2,10},{10,2},{3,11},{11,3},{4,12},{12,4},... | collective-permute-start | bytes 1572872 | tf_op jit(solution)/shard_map/ppermute | solution.py:332
  0.9 10.1 %collective-permute-start = (bf16[2,256,128]{2,1,0:T(8,128)(2,1)S(1)}, bf16[2,256,128]{2,1,0:T(8,128)(2,1)S(1)}, u32[]{:S(2)}, u32[]{:S(2)}) collective-permute-start(bf16[2,256,128]{2,1,0:T(8,128)(2,1)S(1)} %pad_maximum_fusion.own_ref), channel_id=1, source_target_pairs={{0,16},{16,32},{32,48},{48,64},{64,80},{80,96},{96,112},{112,0},{1... | collective-permute-start | bytes 393224 | tf_op jit(solution)/shard_map/ppermute | solution.py:338
  2.9 8.1 %collective-permute-start.5 = (bf16[2,256,128]{2,1,0:T(8,128)(2,1)S(1)}, bf16[2,256,128]{2,1,0:T(8,128)(2,1)S(1)}, u32[]{:S(2)}, u32[]{:S(2)}) collective-permute-start(bf16[2,256,128]{2,1,0:T(8,128)(2,1)S(1)} %pad_maximum_fusion.own_ref), channel_id=1, source_target_pairs={{0,112},{16,0},{32,16},{48,32},{64,48},{80,64},{96,80},{112,96},{1... | collective-permute-start | bytes 393224 | tf_op jit(solution)/shard_map/ppermute | solution.py:340
  11.0 6.5 %collective-permute-start.1 = (bf16[2,256,128]{2,1,0:T(8,128)(2,1)S(1)}, bf16[2,256,128]{2,1,0:T(8,128)(2,1)S(1)}, u32[]{:S(2)}, u32[]{:S(2)}) collective-permute-start(bf16[2,256,128]{2,1,0:T(8,128)(2,1)S(1)} %collective-permute-done.ahead_ref), channel_id=1, source_target_pairs={{0,16},{16,32},{32,48},{48,64},{64,80},{80,96},{96,112},{112,0},{1... | collective-permute-start | bytes 393224 | tf_op jit(solution)/shard_map/ppermute | solution.py:338
  11.0 6.5 %collective-permute-start.6 = (bf16[2,256,128]{2,1,0:T(8,128)(2,1)S(1)}, bf16[2,256,128]{2,1,0:T(8,128)(2,1)S(1)}, u32[]{:S(2)}, u32[]{:S(2)}) collective-permute-start(bf16[2,256,128]{2,1,0:T(8,128)(2,1)S(1)} %collective-permute-done.5.behind_ref), channel_id=1, source_target_pairs={{0,112},{16,0},{32,16},{48,32},{64,48},{80,64},{96,80},{112,96},{1... | collective-permute-start | bytes 393224 | tf_op jit(solution)/shard_map/ppermute | solution.py:340
  17.5 8.6 %collective-permute-start.2 = (bf16[2,256,128]{2,1,0:T(8,128)(2,1)S(1)}, bf16[2,256,128]{2,1,0:T(8,128)(2,1)S(1)}, u32[]{:S(2)}, u32[]{:S(2)}) collective-permute-start(bf16[2,256,128]{2,1,0:T(8,128)(2,1)S(1)} %collective-permute-done.1.ahead_ref), channel_id=1, source_target_pairs={{0,16},{16,32},{32,48},{48,64},{64,80},{80,96},{96,112},{112,0},{1... | collective-permute-start | bytes 393224 | tf_op jit(solution)/shard_map/ppermute | solution.py:338
  17.5 8.6 %collective-permute-start.7 = (bf16[2,256,128]{2,1,0:T(8,128)(2,1)S(1)}, bf16[2,256,128]{2,1,0:T(8,128)(2,1)S(1)}, u32[]{:S(2)}, u32[]{:S(2)}) collective-permute-start(bf16[2,256,128]{2,1,0:T(8,128)(2,1)S(1)} %collective-permute-done.6.behind_ref), channel_id=1, source_target_pairs={{0,112},{16,0},{32,16},{48,32},{64,48},{80,64},{96,80},{112,96},{1... | collective-permute-start | bytes 393224 | tf_op jit(solution)/shard_map/ppermute | solution.py:340
  20.8 1.0 %copy-start = (bf16[256,1024]{1,0:T(8,128)(2,1)S(1)}, bf16[256,1024]{1,0:T(8,128)(2,1)}, u32[]{:S(2)}) copy-start(bf16[256,1024]{1,0:T(8,128)(2,1)} %queries_ref.1) | copy-start | bytes 1572868
  24.8 18.9 %slice-start = ((s8[8388608]{0:T(1024)(128)(4,1)}), s8[4194304]{0:T(1024)(128)(4,1)S(1)}, s32[]{:S(2)}) async-start(s8[8388608]{0:T(1024)(128)(4,1)} %bitcast.6), calls=%async_computation | async-start | bytes 8388608
  25.5 18.1 %slice-start.1 = ((s8[8388608]{0:T(1024)(128)(4,1)}), s8[4194304]{0:T(1024)(128)(4,1)S(1)}, s32[]{:S(2)}) async-start(s8[8388608]{0:T(1024)(128)(4,1)} %bitcast.6), calls=%async_computation.1 | async-start | bytes 8388608
  27.0 15.9 %collective-permute-start.9 = (bf16[8,128,256]{2,1,0:T(8,128)(2,1)S(1)}, bf16[8,128,256]{2,1,0:T(8,128)(2,1)S(1)}, u32[]{:S(2)}, u32[]{:S(2)}) collective-permute-start(bf16[8,128,256]{2,1,0:T(8,128)(2,1)S(1)} %get-tuple-element.52), channel_id=1, source_target_pairs={{0,8},{8,0},{1,9},{9,1},{2,10},{10,2},{3,11},{11,3},{4,12},{12,4},... | collective-permute-start | bytes 1572872 | tf_op jit(solution)/shard_map/ppermute | solution.py:332
  27.1 14.4 %collective-permute-start.3 = (bf16[2,256,128]{2,1,0:T(8,128)(2,1)S(1)}, bf16[2,256,128]{2,1,0:T(8,128)(2,1)S(1)}, u32[]{:S(2)}, u32[]{:S(2)}) collective-permute-start(bf16[2,256,128]{2,1,0:T(8,128)(2,1)S(1)} %collective-permute-done.2.ahead_ref), channel_id=1, source_target_pairs={{0,16},{16,32},{32,48},{48,64},{64,80},{80,96},{96,112},{112,0},{1... | collective-permute-start | bytes 393224 | tf_op jit(solution)/shard_map/ppermute | solution.py:338
  41.5 2.1 %collective-permute-start.4 = (bf16[2,256,128]{2,1,0:T(8,128)(2,1)S(1)}, bf16[2,256,128]{2,1,0:T(8,128)(2,1)S(1)}, u32[]{:S(2)}, u32[]{:S(2)}) collective-permute-start(bf16[2,256,128]{2,1,0:T(8,128)(2,1)S(1)} %collective-permute-done.3.ahead_ref), channel_id=1, source_target_pairs={{0,8},{8,0},{1,9},{9,1},{2,10},{10,2},{3,11},{11,3},{4,12},{12,4},... | collective-permute-start | bytes 393224 | tf_op jit(solution)/shard_map/ppermute | solution.py:332
  41.5 1.4 %collective-permute-start.10 = (f32[2,8,1,256]{3,2,1,0:T(1,128)S(1)}, f32[2,8,1,256]{3,2,1,0:T(1,128)S(1)}, u32[]{:S(2)}, u32[]{:S(2)}) collective-permute-start(f32[2,8,1,256]{3,2,1,0:T(1,128)S(1)} %get-tuple-element.53), channel_id=1, source_target_pairs={{0,8},{8,0},{1,9},{9,1},{2,10},{10,2},{3,11},{11,3},{4,12},{12,4},... | collective-permute-start | bytes 49160 | tf_op jit(solution)/shard_map/ppermute | solution.py:332
  45.7 19.7 %collective-permute-start.11 = (bf16[4,128,512]{2,1,0:T(8,128)(2,1)S(1)}, bf16[4,128,512]{2,1,0:T(8,128)(2,1)S(1)}, u32[]{:S(2)}, u32[]{:S(2)}) collective-permute-start(bf16[4,128,512]{2,1,0:T(8,128)(2,1)S(1)} %get-tuple-element.62), channel_id=1, source_target_pairs={{0,1},{1,0},{2,3},{3,2},{4,5},{5,4},{6,7},{7,6},{8,9},{9,8},{10,11... | collective-permute-start | bytes 1572872 | tf_op jit(solution)/shard_map/ppermute | solution.py:351
  48.6 10.8 %collective-permute-start.15 = (bf16[2,128,512]{2,1,0:T(8,128)(2,1)S(1)}, bf16[2,128,512]{2,1,0:T(8,128)(2,1)S(1)}, u32[]{:S(2)}, u32[]{:S(2)}) collective-permute-start(bf16[2,128,512]{2,1,0:T(8,128)(2,1)S(1)} %get-tuple-element.68), channel_id=1, source_target_pairs={{0,4},{2,6},{4,0},{6,2},{1,5},{3,7},{5,1},{7,3},{8,12},{10,14},{12... | collective-permute-start | bytes 786440 | tf_op jit(solution)/shard_map/ppermute | solution.py:352
  51.9 12.2 %collective-permute-start.16 = (bf16[2,128,512]{2,1,0:T(8,128)(2,1)S(1)}, bf16[2,128,512]{2,1,0:T(8,128)(2,1)S(1)}, u32[]{:S(2)}, u32[]{:S(2)}) collective-permute-start(bf16[2,128,512]{2,1,0:T(8,128)(2,1)S(1)} %get-tuple-element.69), channel_id=1, source_target_pairs={{0,2},{2,4},{4,6},{6,0},{1,3},{3,5},{5,7},{7,1},{8,10},{10,12},{12... | collective-permute-start | bytes 786440 | tf_op jit(solution)/shard_map/ppermute | solution.py:352
  52.6 11.9 %collective-permute-start.17 = (bf16[2,128,512]{2,1,0:T(8,128)(2,1)S(1)}, bf16[2,128,512]{2,1,0:T(8,128)(2,1)S(1)}, u32[]{:S(2)}, u32[]{:S(2)}) collective-permute-start(bf16[2,128,512]{2,1,0:T(8,128)(2,1)S(1)} %get-tuple-element.70), channel_id=1, source_target_pairs={{0,6},{2,0},{4,2},{6,4},{1,7},{3,1},{5,3},{7,5},{8,14},{10,8},{12,... | collective-permute-start | bytes 786440 | tf_op jit(solution)/shard_map/ppermute | solution.py:352
  64.6 6.4 %collective-permute-start.18 = (bf16[128,512]{1,0:T(8,128)(2,1)S(1)}, bf16[128,512]{1,0:T(8,128)(2,1)S(1)}, u32[]{:S(2)}, u32[]{:S(2)}) collective-permute-start(bf16[128,512]{1,0:T(8,128)(2,1)S(1)} %get-tuple-element.72), channel_id=1, source_target_pairs={{0,1},{1,0},{2,3},{3,2},{4,5},{5,4},{6,7},{7,6},{8,9},{9,8},{10,11... | collective-permute-start | bytes 393224 | tf_op jit(solution)/shard_map/ppermute | solution.py:351
  65.6 7.7 %collective-permute-start.12 = (bf16[128,512]{1,0:T(8,128)(2,1)S(1)}, bf16[128,512]{1,0:T(8,128)(2,1)S(1)}, u32[]{:S(2)}, u32[]{:S(2)}) collective-permute-start(bf16[128,512]{1,0:T(8,128)(2,1)S(1)} %get-tuple-element.64), channel_id=1, source_target_pairs={{0,4},{2,6},{4,0},{6,2},{1,5},{3,7},{5,1},{7,3},{8,12},{10,14},{12... | collective-permute-start | bytes 393224 | tf_op jit(solution)/shard_map/ppermute | solution.py:352
  67.7 7.0 %collective-permute-start.13 = (bf16[128,512]{1,0:T(8,128)(2,1)S(1)}, bf16[128,512]{1,0:T(8,128)(2,1)S(1)}, u32[]{:S(2)}, u32[]{:S(2)}) collective-permute-start(bf16[128,512]{1,0:T(8,128)(2,1)S(1)} %get-tuple-element.65), channel_id=1, source_target_pairs={{0,2},{2,4},{4,6},{6,0},{1,3},{3,5},{5,7},{7,1},{8,10},{10,12},{12... | collective-permute-start | bytes 393224 | tf_op jit(solution)/shard_map/ppermute | solution.py:352
  69.2 5.9 %collective-permute-start.14 = (bf16[128,512]{1,0:T(8,128)(2,1)S(1)}, bf16[128,512]{1,0:T(8,128)(2,1)S(1)}, u32[]{:S(2)}, u32[]{:S(2)}) collective-permute-start(bf16[128,512]{1,0:T(8,128)(2,1)S(1)} %get-tuple-element.66), channel_id=1, source_target_pairs={{0,6},{2,0},{4,2},{6,4},{1,7},{3,1},{5,3},{7,5},{8,14},{10,8},{12,... | collective-permute-start | bytes 393224 | tf_op jit(solution)/shard_map/ppermute | solution.py:352

commit v2 on v1

--- a/solution.py
+++ b/solution.py
@@ -8,7 +8,7 @@
 
 HD = 128
 SIDE = 4
-AWAY = (2, 1, 3)
+AWAY = (1, 3, 2)
 LOWEST = -1e30
 LOG2E = 1.4426950408889634
 SCALE = LOG2E * HD ** (-0.5)
@@ -46,19 +46,7 @@
     def scores_of(h):
         return jnp.dot(keys, q_ref[h], preferred_element_type=jnp.float32) * SCALE
 
-    ahead = scores_of(0)
-    for h in range(heads):
-        scores = ahead
-        if h + 1 < heads:
-            ahead = scores_of(h + 1)
-        if diag:
-            scores = jnp.where(keep, scores, -jnp.inf)
-        top = jnp.max(scores, axis=0, keepdims=True)
-        if not first:
-            old = top_ref[h]
-            top = jnp.maximum(old, top)
-            shrink = jnp.exp2(old - top)
-        weights = jnp.exp2(scores - top).astype(jnp.bfloat16)
+    def settle(h, weights, top, shrink):
         both = jnp.dot(values_t, weights, preferred_element_type=jnp.float32)
         acc, total = both[:HD], both[HD : HD + 1]
         top_ref[h] = top
@@ -69,9 +57,34 @@
             sum_ref[h] = sum_ref[h] * shrink + total
             acc_ref[h] = acc_ref[h] * shrink + acc
 
+    ahead = [scores_of(h) for h in range(2)]
+    waiting = None
+    for h in range(heads):
+        scores = ahead.pop(0)
+        if h + 2 < heads:
+            ahead.append(scores_of(h + 2))
+        if diag:
+            scores = jnp.where(keep, scores, -jnp.inf)
+        top = jnp.max(scores, axis=0, keepdims=True)
+        shrink = None
+        if not first:
+            old = top_ref[h]
+            top = jnp.maximum(old, top)
+            shrink = jnp.exp2(old - top)
+        weights = jnp.exp2(scores - top).astype(jnp.bfloat16)
+        if waiting:
+            settle(*waiting)
+        waiting = (h, weights, top, shrink)
+    settle(*waiting)
+
 
 def sds(shape, dtype):
     return jax.ShapeDtypeStruct(shape, dtype)
+
+
+def turned(queries_ref, out_ref):
+    for h in range(out_ref.shape[0]):
+        out_ref[h] = queries_ref[:, h * HD : (h + 1) * HD].T
 
 
 def open_state(where, queries, others, own):
@@ -79,11 +92,11 @@
     heads = width // HD
 
     def kernel(where_ref, queries_ref, others_ref, own_ref, *state):
-        for h in range(heads):
-            state[0][h] = queries_ref[:, h * HD : (h + 1) * HD].T
-            state[0][heads + h] = others_ref[:, h * HD : (h + 1) * HD].T
-        absorb([own_ref], [r.at[:heads] for r in state], first=True, diag=True)
+        live = [r.at[:heads] for r in state]
         rest = [r.at[heads:] for r in state]
+        turned(queries_ref, live[0])
+        turned(others_ref, rest[0])
+        absorb([own_ref], live, first=True, diag=True)
 
         @pl.when(where_ref[1] == 0)
         def _():
@@ -111,9 +124,9 @@
     )(where, queries, others, own)
 
 
-def fold(where, state, ahead, behind, step, parting):
+def fold(where, state, ahead, behind, step, parting=False, heads=None):
     def kernel(where_ref, ahead_ref, behind_ref, *refs):
-        live = refs[:4]
+        live = refs[:4] if heads is None else [r.at[:heads] for r in refs[:4]]
         z = where_ref[0]
         size = where_ref[2]
 
@@ -123,20 +136,24 @@
 
         @pl.when((z + step < size) & (z >= step))
         def _():
-            absorb([ahead_ref], live)
+            def part(i, _):
+                absorb([ahead_ref], [r.at[pl.ds(i * 4, 4)] for r in live])
+                return 0
+
+            lax.fori_loop(0, live[1].shape[0] // 4, part, 0)
 
         if parting:
             out_ref, stat_ref = refs[-2:]
-            heads = live[0].shape[0] // 2
-            for h in range(heads):
-                total = live[2][heads + h]
+            half = live[0].shape[0] // 2
+            for h in range(half):
+                total = live[2][half + h]
                 scale = jnp.where(total > 0, 1.0 / jnp.where(total > 0, total, 1.0), 0.0)
-                out_ref[h] = (live[3][heads + h] * scale).astype(jnp.bfloat16)
-                stat_ref[0, h] = live[1][heads + h]
+                out_ref[h] = (live[3][half + h] * scale).astype(jnp.bfloat16)
+                stat_ref[0, h] = live[1][half + h]
                 stat_ref[1, h] = total
 
-    heads, _, rows = state[0].shape
-    extra = (sds((heads // 2, HD, rows), jnp.bfloat16), sds((2, heads // 2, 1, rows), jnp.float32)) if parting else ()
+    full, _, rows = state[0].shape
+    extra = (sds((full // 2, HD, rows), jnp.bfloat16), sds((2, full // 2, 1, rows), jnp.float32)) if parting else ()
     out = pl.pallas_call(
         kernel,
         out_shape=tuple(sds(a.shape, a.dtype) for a in state) + extra,
@@ -144,7 +161,7 @@
         out_specs=(VMEM,) * (4 + len(extra)),
         input_output_aliases={3 + i: i for i in range(4)},
         compiler_params=params(),
-        cost_estimate=cost(2 * ahead.shape[1], rows, heads),
+        cost_estimate=cost(2 * ahead.shape[1], rows, heads or full),
     )(where, ahead, behind, *state)
     return (out[:4], out[4:]) if parting else out
 
@@ -202,7 +219,7 @@
             absorb([ahead_ref], live)
 
         for h in range(heads):
-            att_ref[:, h * HD : (h + 1) * HD] = (live[3][h] / live[2][h]).T.astype(jnp.bfloat16)
+            att_ref[:, h * HD : (h + 1) * HD] = (live[3][h] * (1.0 / live[2][h])).astype(jnp.bfloat16).T
 
         def one(d, _):
             start = column(where_ref, d, 1, width)
@@ -330,19 +347,24 @@
     up = [(i, (i + 1) % chips) for i in range(chips)]
     down = [(i, (i - 1) % chips) for i in range(chips)]
     swap = lambda a: lax.ppermute(a, "core", [(0, 1), (1, 0)])
+    own = jnp.stack([keys, values])
     others = swap(queries)
-    own = jnp.stack([keys, values])
     half = chips // 2
+    heads = queries.shape[1] // HD
     ahead, behind = [own], [own]
     for k in range(1, half + 1):
         ahead.append(lax.ppermute(ahead[-1], "z", up))
         if k < half:
             behind.append(lax.ppermute(behind[-1], "z", down))
     state = open_state(where, queries, others, own)
-    for k in range(1, half):
-        state = fold(where, state, ahead[k], behind[k], k, k + 1 == half)
+    for k in range(1, half - 1):
+        state = fold(where, state, ahead[k], behind[k], k, k + 2 == half)
     state, (parted, stats) = state
+    k = half - 1
+    swap_ahead, swap_behind = swap(ahead[k]), swap(behind[k])
     parted, stats = swap(parted), swap(stats)
+    state = fold(where, state, ahead[k], behind[k], k, heads=heads)
+    state = fold(where, state, swap_ahead, swap_behind, k, heads=heads)
     last = swap(ahead[half])
     mine = join(where, state, parted, stats, ahead[half], half)
     width = out_weight.shape[1] // (2 * SIDE)

time: 76 us -> 74.3 us (0.978)
  the two profiles are of different devices: /device:TPU:4 before, /device:TPU:132 now
where the time goes in v2:
time: 74.3 us; the launch traced here: 74.1 us
  waiting for transfers between devices  28.1 us (38%)
  starting transfers between devices  22.3 us (30%)
  Pallas kernels  21.5 us (29%)
  local copies, waits for them, and re-layouts  1.14 us (2%)
  other arithmetic  0.89 us (1%)
    ppermute x6, waiting for transfers between devices, steps(): lax.ppermute(a, 'y', [(i, (i + d) % SIDE) for i in range(SIDE)])  14.2 us
    ppermute x4, waiting for transfers between devices, steps(): ahead.append(lax.ppermute(ahead[-1], 'z', up))  13.3 us
    pallas_call x4, Pallas kernels, fold(): pl.pallas_call(kernel, out_shape=tuple((sds(a.shape, a.dtype) for a in st...  9.48 us
    ppermute x6, starting transfers between devices, steps(): lax.ppermute(a, 'y', [(i, (i + d) % SIDE) for i in range(SIDE)])  8.93 us
    ppermute x3, starting transfers between devices, steps(): behind.append(lax.ppermute(behind[-1], 'z', down))  8.68 us
    pallas_call x1, Pallas kernels, close(): pl.pallas_call(kernel, out_shape=(sds((rows, heads * HD), jnp.bfloat16),...  3.09 us
    pallas_call x1, Pallas kernels, open_state(): pl.pallas_call(kernel, out_shape=(sds((2 * heads, HD, rows), jnp.bfloat16...  2.39 us
    pallas_call x1, Pallas kernels, project_here(): pl.pallas_call(kernel, out_shape=(sds((2, rows, width), jnp.float32), sds...  2.29 us
  transfers between devices with their start and end apart: 21, of which 10 were waited for; matrix products, arithmetic and copies ran while one was open for 1% of the time, Pallas kernels for 20%

profile of v2, /device:TPU:132, one launch (start us, length us, event | category | flops | bytes accessed | tf_op | source)
XLA Modules:
  0.0 74.1 jit_solution(4870690961389293629)
XLA Ops:
  2.0 2.2 %collective-permute-start.6 = (bf16[2,256,128]{2,1,0:T(8,128)(2,1)S(1)}, bf16[2,256,128]{2,1,0:T(8,128)(2,1)S(1)}, u32[]{:S(2)}, u32[]{:S(2)}) collective-permute-start(bf16[2,256,128]{2,1,0:T(8,128)(2,1)S(1)} %pad_maximum_fusion.own_ref), channel_id=1, source_target_pairs={{0,112},{16,0},{32,16},{48,32},{64,48},{80,64},{96,80},{112,96},{1... | collective-permute-start | bytes 393224 | tf_op jit(solution)/shard_map/ppermute | solution.py:358
  4.3 3.8 %collective-permute-done.ahead_ref = bf16[2,256,128]{2,1,0:T(8,128)(2,1)S(1)} collective-permute-done((bf16[2,256,128]{2,1,0:T(8,128)(2,1)S(1)}, bf16[2,256,128]{2,1,0:T(8,128)(2,1)S(1)}, u32[]{:S(2)}, u32[]{:S(2)}) %collective-permute-start) | collective-permute-done | bytes 131104 | tf_op jit(solution)/shard_map/ppermute | solution.py:356
  8.1 3.2 %collective-permute-start.7 = (bf16[2,256,128]{2,1,0:T(8,128)(2,1)S(1)}, bf16[2,256,128]{2,1,0:T(8,128)(2,1)S(1)}, u32[]{:S(2)}, u32[]{:S(2)}) collective-permute-start(bf16[2,256,128]{2,1,0:T(8,128)(2,1)S(1)} %collective-permute-done.6.behind_ref), channel_id=1, source_target_pairs={{0,112},{16,0},{32,16},{48,32},{64,48},{80,64},{96,80},{112,96},{1... | collective-permute-start | bytes 393224 | tf_op jit(solution)/shard_map/ppermute | solution.py:358
  12.4 2.4 %open_state.1 = (bf16[16,128,256]{2,1,0:T(8,128)(2,1)S(1)}, f32[16,1,256]{2,1,0:T(1,128)S(1)}, f32[16,1,256]{2,1,0:T(1,128)S(1)}, f32[16,128,256]{2,1,0:T(8,128)S(1)}) custom-call(s32[5]{0:T(128)S(1)} %stack.28.where_ref, bf16[256,1024]{1,0:T(8,128)(2,1)S(1)} %copy-done, bf16[256,1024]{1,0:T(8,128)(2,1)S(1)} %collective-permute-done.10.others_ref, ...), custom_call_target="tpu_custom_call" | custom-call | flops 536870912 | bytes 2228224 | tf_op jit(solution)/shard_map/open_state/pallas_call | solution.py:111
  14.8 3.0 %shard_map.46 = (bf16[16,128,256]{2,1,0:T(8,128)(2,1)S(1)}, f32[16,1,256]{2,1,0:T(1,128)S(1)}, f32[16,1,256]{2,1,0:T(1,128)S(1)}, f32[16,128,256]{2,1,0:T(8,128)S(1)}) custom-call(s32[5]{0:T(128)S(1)} %stack.28.where_ref, ...), custom_call_target="tpu_custom_call", output_to_operand_aliasing={{0}: (3, {}), {1}: (4, {}), {2}: (5, {}), {3}: (6, {})} | custom-call | flops 1073741824 | bytes 2359296 | tf_op jit(solution)/shard_map/pallas_call | solution.py:157
  17.8 3.0 %shard_map.47 = (bf16[16,128,256]{2,1,0:T(8,128)(2,1)S(1)}, f32[16,1,256]{2,1,0:T(1,128)S(1)}, f32[16,1,256]{2,1,0:T(1,128)S(1)}, f32[16,128,256]{2,1,0:T(8,128)...) custom-call(s32[5]{0:T(128)S(1)} %stack.28.where_ref, ...), custom_call_target="tpu_custom_call", output_to_operand_aliasing={{0}: (3, {}), {1}: (4, {}), {2}: (5, {}), {3}: (6, {})} | custom-call | flops 1073741824 | bytes 2359296 | tf_op jit(solution)/shard_map/pallas_call | solution.py:157
  21.2 3.2 %collective-permute-start.8 = (bf16[2,256,128]{2,1,0:T(8,128)(2,1)S(1)}, bf16[2,256,128]{2,1,0:T(8,128)(2,1)S(1)}, u32[]{:S(2)}, u32[]{:S(2)}) collective-permute-start(bf16[2,256,128]{2,1,0:T(8,128)(2,1)S(1)} %collective-permute-done.7.behind_ref), channel_id=1, source_target_pairs={{0,112},{16,0},{32,16},{48,32},{64,48},{80,64},{96,80},{112,96},{1... | collective-permute-start | bytes 393224 | tf_op jit(solution)/shard_map/ppermute | solution.py:358
  24.4 3.8 %collective-permute-done.2.ahead_ref = bf16[2,256,128]{2,1,0:T(8,128)(2,1)S(1)} collective-permute-done((bf16[2,256,128]{2,1,0:T(8,128)(2,1)S(1)}, bf16[2,256,128]{2,1,0:T(8,128)(2,1)S(1)}, u32[]{:S(2)}, u32[]{:S(2)}) %collective-permute-start.2) | collective-permute-done | bytes 131104 | tf_op jit(solution)/shard_map/ppermute | solution.py:356
  28.7 5.7 %collective-permute-done.3.ahead_ref = bf16[2,256,128]{2,1,0:T(8,128)(2,1)S(1)} collective-permute-done((bf16[2,256,128]{2,1,0:T(8,128)(2,1)S(1)}, bf16[2,256,128]{2,1,0:T(8,128)(2,1)S(1)}, u32[]{:S(2)}, u32[]{:S(2)}) %collective-permute-start.3) | collective-permute-done | bytes 131104 | tf_op jit(solution)/shard_map/ppermute | solution.py:356
  34.9 1.7 %shard_map.48 = (bf16[16,128,256]{2,1,0:T(8,128)(2,1)S(1)}, f32[16,1,256]{2,1,0:T(1,128)S(1)}, f32[16,1,256]{2,1,0:T(1,128)S(1)}, f32[16,128,256]{2,1,0:T(8,128)S(1)}) custom-call(s32[5]{0:T(128)S(1)} %stack.28.where_ref, ...), custom_call_target="tpu_custom_call", output_to_operand_aliasing={{0}: (3, {}), {1}: (4, {}), {2}: (5, {}), {3}: (6, {})} | custom-call | flops 536870912 | bytes 1310720 | tf_op jit(solution)/shard_map/pallas_call | solution.py:157
  36.7 1.8 %shard_map.49 = (bf16[16,128,256]{2,1,0:T(8,128)(2,1)S(1)}, f32[16,1,256]{2,1,0:T(1,128)S(1)}, f32[16,1,256]{2,1,0:T(1,128)S(1)}, f32[16,128,256]{2,1,0:T(8,128)S(1)}) custom-call(s32[5]{0:T(128)S(1)} %stack.28.where_ref, ...), custom_call_target="tpu_custom_call", output_to_operand_aliasing={{0}: (3, {}), {1}: (4, {}), {2}: (5, {}), {3}: (6, {})} | custom-call | flops 536870912 | bytes 1310720 | tf_op jit(solution)/shard_map/pallas_call | solution.py:157
  38.4 1.7 %join.1 = (f32[8,1,256]{2,1,0:T(1,128)S(1)}, f32[8,1,256]{2,1,0:T(1,128)S(1)}, f32[8,128,256]{2,1,0:T(8,128)S(1)}) custom-call(s32[5]{0:T(128)S(1)} %stack.28.where_ref, bf16[8,128,256]{2,1,0:T(8,128)(2,1)S(1)} %collective-permute-done.11.parted_ref, f32[2,8,1,256]{3,2,1,0:T(1,128)S(1)} %collective-permute-done.12.stats_ref, ...), custom_call_target="tpu_custom_call" | custom-call | flops 268435456 | bytes 1179648 | tf_op jit(solution)/shard_map/join/pallas_call | solution.py:188
  40.2 3.1 %close.1 = (bf16[256,1024]{1,0:T(8,128)(2,1)S(1)}, bf16[4,128,512]{2,1,0:T(8,128)(2,1)S(1)}) custom-call(s32[5]{0:T(128)S(1)} %stack.28.where_ref, bf16[2,256,128]{2,1,0:T(8,128)(2,1)S(1)} %collective-permute-done.4.ahead_ref, bf16[16,128,256]{2,1,0:T(8,128)(2,1)S(1)} %get-tuple-element.59.refs_0_.q_ref, f32[8,1,256]{2,1,0:T(1,128)S(1)} %get-tuple-element.65.top_ref, ...), custom_call_target="tpu_custom_call" | custom-call | flops 536870912 | bytes 1310720 | tf_op jit(solution)/shard_map/close/pallas_call | solution.py:231
  44.6 1.6 %project_away.1 = (bf16[2,128,512]{2,1,0:T(8,128)(2,1)S(1)}, bf16[2,128,512]{2,1,0:T(8,128)(2,1)S(1)}, bf16[2,128,512]{2,1,0:T(8,128)(2,1)S(1)}) custom-call(s32[5]{0:T(128)S(1)} %stack.28.where_ref, bf16[256,1024]{1,0:T(8,128)(2,1)S(1)} %get-tuple-element.68.att_ref, bf16[1024,4096]{1,0:T(8,128)(2,1)S(1)} %bitcast.7), custom_call_target="tpu_custom_call" | custom-call | flops 134217728 | bytes 655360 | tf_op jit(solution)/shard_map/project_away/pallas_call | solution.py:252
  46.1 1.9 %collective-permute-start.17 = (bf16[2,128,512]{2,1,0:T(8,128)(2,1)S(1)}, bf16[2,128,512]{2,1,0:T(8,128)(2,1)S(1)}, u32[]{:S(2)}, u32[]{:S(2)}) collective-permute-start(bf16[2,128,512]{2,1,0:T(8,128)(2,1)S(1)} %get-tuple-element.76), channel_id=1, source_target_pairs={{0,2},{2,4},{4,6},{6,0},{1,3},{3,5},{5,7},{7,1},{8,10},{10,12},{12... | collective-permute-start | bytes 786440 | tf_op jit(solution)/shard_map/ppermute | solution.py:374
  48.0 1.7 %collective-permute-start.18 = (bf16[2,128,512]{2,1,0:T(8,128)(2,1)S(1)}, bf16[2,128,512]{2,1,0:T(8,128)(2,1)S(1)}, u32[]{:S(2)}, u32[]{:S(2)}) collective-permute-start(bf16[2,128,512]{2,1,0:T(8,128)(2,1)S(1)} %get-tuple-element.77), channel_id=1, source_target_pairs={{0,6},{2,0},{4,2},{6,4},{1,7},{3,1},{5,3},{7,5},{8,14},{10,8},{12,... | collective-permute-start | bytes 786440 | tf_op jit(solution)/shard_map/ppermute | solution.py:374
  49.7 2.0 %collective-permute-start.19 = (bf16[2,128,512]{2,1,0:T(8,128)(2,1)S(1)}, bf16[2,128,512]{2,1,0:T(8,128)(2,1)S(1)}, u32[]{:S(2)}, u32[]{:S(2)}) collective-permute-start(bf16[2,128,512]{2,1,0:T(8,128)(2,1)S(1)} %get-tuple-element.78), channel_id=1, source_target_pairs={{0,4},{2,6},{4,0},{6,2},{1,5},{3,7},{5,1},{7,3},{8,12},{10,14},{12... | collective-permute-start | bytes 786440 | tf_op jit(solution)/shard_map/ppermute | solution.py:374
  51.7 2.3 %project_here.1 = (f32[2,128,512]{2,1,0:T(8,128)S(1)}, f32[4,128,512]{2,1,0:T(8,128)S(1)}) custom-call(s32[5]{0:T(128)S(1)} %stack.28.where_ref, bf16[256,1024]{1,0:T(8,128)(2,1)S(1)} %get-tuple-element.68.att_ref, bf16[1024,4096]{1,0:T(8,128)(2,1)S(1)} %bitcast.7), custom_call_target="tpu_custom_call" | custom-call | flops 134217728 | bytes 655360 | tf_op jit(solution)/shard_map/project_here/pallas_call | solution.py:276
  54.0 1.8 %collective-permute-done.17.refs_0_ = bf16[2,128,512]{2,1,0:T(8,128)(2,1)S(1)} collective-permute-done((bf16[2,128,512]{2,1,0:T(8,128)(2,1)S(1)}, bf16[2,128,512]{2,1,0:T(8,128)(2,1)S(1)}, u32[]{:S(2)}, u32[]{:S(2)}) %collective-permute-start.17) | collective-permute-done | bytes 262176 | tf_op jit(solution)/shard_map/ppermute | solution.py:374
  55.7 4.9 %collective-permute-done.18.refs_1_ = bf16[2,128,512]{2,1,0:T(8,128)(2,1)S(1)} collective-permute-done((bf16[2,128,512]{2,1,0:T(8,128)(2,1)S(1)}, bf16[2,128,512]{2,1,0:T(8,128)(2,1)S(1)}, u32[]{:S(2)}, u32[]{:S(2)}) %collective-permute-start.18) | collective-permute-done | bytes 262176 | tf_op jit(solution)/shard_map/ppermute | solution.py:374
  60.6 1.8 %collective-permute-done.19.refs_2_ = bf16[2,128,512]{2,1,0:T(8,128)(2,1)S(1)} collective-permute-done((bf16[2,128,512]{2,1,0:T(8,128)(2,1)S(1)}, bf16[2,128,512]{2,1,0:T(8,128)(2,1)S(1)}, u32[]{:S(2)}, u32[]{:S(2)}) %collective-permute-start.19) | collective-permute-done | bytes 262176 | tf_op jit(solution)/shard_map/ppermute | solution.py:374
  64.8 2.1 %collective-permute-start.15 = (bf16[128,512]{1,0:T(8,128)(2,1)S(1)}, bf16[128,512]{1,0:T(8,128)(2,1)S(1)}, u32[]{:S(2)}, u32[]{:S(2)}) collective-permute-start(bf16[128,512]{1,0:T(8,128)(2,1)S(1)} %get-tuple-element.73), channel_id=1, source_target_pairs={{0,6},{2,0},{4,2},{6,4},{1,7},{3,1},{5,3},{7,5},{8,14},{10,8},{12,... | collective-permute-start | bytes 393224 | tf_op jit(solution)/shard_map/ppermute | solution.py:374
  67.6 3.0 %collective-permute-done.14.refs_0_ = bf16[128,512]{1,0:T(8,128)(2,1)S(1)} collective-permute-done((bf16[128,512]{1,0:T(8,128)(2,1)S(1)}, bf16[128,512]{1,0:T(8,128)(2,1)S(1)}, u32[]{:S(2)}, u32[]{:S(2)}) %collective-permute-start.14) | collective-permute-done | bytes 131104 | tf_op jit(solution)/shard_map/ppermute | solution.py:374
  70.9 2.4 %collective-permute-done.16.refs_2_ = bf16[128,512]{1,0:T(8,128)(2,1)S(1)} collective-permute-done((bf16[128,512]{1,0:T(8,128)(2,1)S(1)}, bf16[128,512]{1,0:T(8,128)(2,1)S(1)}, u32[]{:S(2)}, u32[]{:S(2)}) %collective-permute-start.16) | collective-permute-done | bytes 131104 | tf_op jit(solution)/shard_map/ppermute | solution.py:374
  (39 shorter events, 10.0 us)
Async XLA Ops:
  0.0 11.3 %collective-permute-start.10 = (bf16[256,1024]{1,0:T(8,128)(2,1)}, bf16[256,1024]{1,0:T(8,128)(2,1)S(1)}, u32[]{:S(2)}, u32[]{:S(2)}) collective-permute-start(bf16[256,1024]{1,0:T(8,128)(2,1)} %queries_ref.1), channel_id=1, source_target_pairs={{0,8},{8,0},{1,9},{9,1},{2,10},{10,2},{3,11},{11,3},{4,12},{12,4},... | collective-permute-start | bytes 1572872 | tf_op jit(solution)/shard_map/ppermute | solution.py:349
  0.9 7.2 %collective-permute-start = (bf16[2,256,128]{2,1,0:T(8,128)(2,1)S(1)}, bf16[2,256,128]{2,1,0:T(8,128)(2,1)S(1)}, u32[]{:S(2)}, u32[]{:S(2)}) collective-permute-start(bf16[2,256,128]{2,1,0:T(8,128)(2,1)S(1)} %pad_maximum_fusion.own_ref), channel_id=1, source_target_pairs={{0,16},{16,32},{32,48},{48,64},{64,80},{80,96},{96,112},{112,0},{1... | collective-permute-start | bytes 393224 | tf_op jit(solution)/shard_map/ppermute | solution.py:356
  2.0 6.1 %collective-permute-start.6 = (bf16[2,256,128]{2,1,0:T(8,128)(2,1)S(1)}, bf16[2,256,128]{2,1,0:T(8,128)(2,1)S(1)}, u32[]{:S(2)}, u32[]{:S(2)}) collective-permute-start(bf16[2,256,128]{2,1,0:T(8,128)(2,1)S(1)} %pad_maximum_fusion.own_ref), channel_id=1, source_target_pairs={{0,112},{16,0},{32,16},{48,32},{64,48},{80,64},{96,80},{112,96},{1... | collective-permute-start | bytes 393224 | tf_op jit(solution)/shard_map/ppermute | solution.py:358
  8.1 9.7 %collective-permute-start.1 = (bf16[2,256,128]{2,1,0:T(8,128)(2,1)S(1)}, bf16[2,256,128]{2,1,0:T(8,128)(2,1)S(1)}, u32[]{:S(2)}, u32[]{:S(2)}) collective-permute-start(bf16[2,256,128]{2,1,0:T(8,128)(2,1)S(1)} %collective-permute-done.ahead_ref), channel_id=1, source_target_pairs={{0,16},{16,32},{32,48},{48,64},{64,80},{80,96},{96,112},{112,0},{1... | collective-permute-start | bytes 393224 | tf_op jit(solution)/shard_map/ppermute | solution.py:356
  8.1 9.7 %collective-permute-start.7 = (bf16[2,256,128]{2,1,0:T(8,128)(2,1)S(1)}, bf16[2,256,128]{2,1,0:T(8,128)(2,1)S(1)}, u32[]{:S(2)}, u32[]{:S(2)}) collective-permute-start(bf16[2,256,128]{2,1,0:T(8,128)(2,1)S(1)} %collective-permute-done.6.behind_ref), channel_id=1, source_target_pairs={{0,112},{16,0},{32,16},{48,32},{64,48},{80,64},{96,80},{112,96},{1... | collective-permute-start | bytes 393224 | tf_op jit(solution)/shard_map/ppermute | solution.py:358
  11.3 1.0 %copy-start = (bf16[256,1024]{1,0:T(8,128)(2,1)S(1)}, bf16[256,1024]{1,0:T(8,128)(2,1)}, u32[]{:S(2)}) copy-start(bf16[256,1024]{1,0:T(8,128)(2,1)} %queries_ref.1) | copy-start | bytes 1572868
  14.8 25.4 %slice-start = ((s8[8388608]{0:T(1024)(128)(4,1)}), s8[4194304]{0:T(1024)(128)(4,1)S(1)}, s32[]{:S(2)}) async-start(s8[8388608]{0:T(1024)(128)(4,1)} %bitcast.6), calls=%async_computation | async-start | bytes 8388608
  20.8 17.6 %collective-permute-start.11 = (bf16[8,128,256]{2,1,0:T(8,128)(2,1)S(1)}, bf16[8,128,256]{2,1,0:T(8,128)(2,1)S(1)}, u32[]{:S(2)}, u32[]{:S(2)}) collective-permute-start(bf16[8,128,256]{2,1,0:T(8,128)(2,1)S(1)} %get-tuple-element.60), channel_id=1, source_target_pairs={{0,8},{8,0},{1,9},{9,1},{2,10},{10,2},{3,11},{11,3},{4,12},{12,4},... | collective-permute-start | bytes 1572872 | tf_op jit(solution)/shard_map/ppermute | solution.py:349
  21.1 7.1 %collective-permute-start.2 = (bf16[2,256,128]{2,1,0:T(8,128)(2,1)S(1)}, bf16[2,256,128]{2,1,0:T(8,128)(2,1)S(1)}, u32[]{:S(2)}, u32[]{:S(2)}) collective-permute-start(bf16[2,256,128]{2,1,0:T(8,128)(2,1)S(1)} %collective-permute-done.1.ahead_ref), channel_id=1, source_target_pairs={{0,16},{16,32},{32,48},{48,64},{64,80},{80,96},{96,112},{112,0},{1... | collective-permute-start | bytes 393224 | tf_op jit(solution)/shard_map/ppermute | solution.py:356
  21.2 7.0 %collective-permute-start.8 = (bf16[2,256,128]{2,1,0:T(8,128)(2,1)S(1)}, bf16[2,256,128]{2,1,0:T(8,128)(2,1)S(1)}, u32[]{:S(2)}, u32[]{:S(2)}) collective-permute-start(bf16[2,256,128]{2,1,0:T(8,128)(2,1)S(1)} %collective-permute-done.7.behind_ref), channel_id=1, source_target_pairs={{0,112},{16,0},{32,16},{48,32},{64,48},{80,64},{96,80},{112,96},{1... | collective-permute-start | bytes 393224 | tf_op jit(solution)/shard_map/ppermute | solution.py:358
  28.2 6.2 %collective-permute-start.3 = (bf16[2,256,128]{2,1,0:T(8,128)(2,1)S(1)}, bf16[2,256,128]{2,1,0:T(8,128)(2,1)S(1)}, u32[]{:S(2)}, u32[]{:S(2)}) collective-permute-start(bf16[2,256,128]{2,1,0:T(8,128)(2,1)S(1)} %collective-permute-done.2.ahead_ref), channel_id=1, source_target_pairs={{0,16},{16,32},{32,48},{48,64},{64,80},{80,96},{96,112},{112,0},{1... | collective-permute-start | bytes 393224 | tf_op jit(solution)/shard_map/ppermute | solution.py:356
  28.2 8.4 %collective-permute-start.5 = (bf16[2,256,128]{2,1,0:T(8,128)(2,1)S(1)}, bf16[2,256,128]{2,1,0:T(8,128)(2,1)S(1)}, u32[]{:S(2)}, u32[]{:S(2)}) collective-permute-start(bf16[2,256,128]{2,1,0:T(8,128)(2,1)S(1)} %collective-permute-done.2.ahead_ref), channel_id=1, source_target_pairs={{0,8},{8,0},{1,9},{9,1},{2,10},{10,2},{3,11},{11,3},{4,12},{12,4},... | collective-permute-start | bytes 393224 | tf_op jit(solution)/shard_map/ppermute | solution.py:349
  28.2 8.4 %collective-permute-start.9 = (bf16[2,256,128]{2,1,0:T(8,128)(2,1)S(1)}, bf16[2,256,128]{2,1,0:T(8,128)(2,1)S(1)}, u32[]{:S(2)}, u32[]{:S(2)}) collective-permute-start(bf16[2,256,128]{2,1,0:T(8,128)(2,1)S(1)} %collective-permute-done.8.behind_ref), channel_id=1, source_target_pairs={{0,8},{8,0},{1,9},{9,1},{2,10},{10,2},{3,11},{11,3},{4,12},{12,4},... | collective-permute-start | bytes 393224 | tf_op jit(solution)/shard_map/ppermute | solution.py:349
  34.4 5.8 %collective-permute-start.4 = (bf16[2,256,128]{2,1,0:T(8,128)(2,1)S(1)}, bf16[2,256,128]{2,1,0:T(8,128)(2,1)S(1)}, u32[]{:S(2)}, u32[]{:S(2)}) collective-permute-start(bf16[2,256,128]{2,1,0:T(8,128)(2,1)S(1)} %collective-permute-done.3.ahead_ref), channel_id=1, source_target_pairs={{0,8},{8,0},{1,9},{9,1},{2,10},{10,2},{3,11},{11,3},{4,12},{12,4},... | collective-permute-start | bytes 393224 | tf_op jit(solution)/shard_map/ppermute | solution.py:349
  34.4 4.0 %collective-permute-start.12 = (f32[2,8,1,256]{3,2,1,0:T(1,128)S(1)}, f32[2,8,1,256]{3,2,1,0:T(1,128)S(1)}, u32[]{:S(2)}, u32[]{:S(2)}) collective-permute-start(f32[2,8,1,256]{3,2,1,0:T(1,128)S(1)} %get-tuple-element.61), channel_id=1, source_target_pairs={{0,8},{8,0},{1,9},{9,1},{2,10},{10,2},{3,11},{11,3},{4,12},{12,4},... | collective-permute-start | bytes 49160 | tf_op jit(solution)/shard_map/ppermute | solution.py:349
  34.9 5.3 %slice-start.1 = ((s8[8388608]{0:T(1024)(128)(4,1)}), s8[4194304]{0:T(1024)(128)(4,1)S(1)}, s32[]{:S(2)}) async-start(s8[8388608]{0:T(1024)(128)(4,1)} %bitcast.6), calls=%async_computation.1 | async-start | bytes 8388608
  43.3 20.2 %collective-permute-start.13 = (bf16[4,128,512]{2,1,0:T(8,128)(2,1)S(1)}, bf16[4,128,512]{2,1,0:T(8,128)(2,1)S(1)}, u32[]{:S(2)}, u32[]{:S(2)}) collective-permute-start(bf16[4,128,512]{2,1,0:T(8,128)(2,1)S(1)} %get-tuple-element.70), channel_id=1, source_target_pairs={{0,1},{1,0},{2,3},{3,2},{4,5},{5,4},{6,7},{7,6},{8,9},{9,8},{10,11... | collective-permute-start | bytes 1572872 | tf_op jit(solution)/shard_map/ppermute | solution.py:373
  46.1 9.6 %collective-permute-start.17 = (bf16[2,128,512]{2,1,0:T(8,128)(2,1)S(1)}, bf16[2,128,512]{2,1,0:T(8,128)(2,1)S(1)}, u32[]{:S(2)}, u32[]{:S(2)}) collective-permute-start(bf16[2,128,512]{2,1,0:T(8,128)(2,1)S(1)} %get-tuple-element.76), channel_id=1, source_target_pairs={{0,2},{2,4},{4,6},{6,0},{1,3},{3,5},{5,7},{7,1},{8,10},{10,12},{12... | collective-permute-start | bytes 786440 | tf_op jit(solution)/shard_map/ppermute | solution.py:374
  48.0 12.6 %collective-permute-start.18 = (bf16[2,128,512]{2,1,0:T(8,128)(2,1)S(1)}, bf16[2,128,512]{2,1,0:T(8,128)(2,1)S(1)}, u32[]{:S(2)}, u32[]{:S(2)}) collective-permute-start(bf16[2,128,512]{2,1,0:T(8,128)(2,1)S(1)} %get-tuple-element.77), channel_id=1, source_target_pairs={{0,6},{2,0},{4,2},{6,4},{1,7},{3,1},{5,3},{7,5},{8,14},{10,8},{12,... | collective-permute-start | bytes 786440 | tf_op jit(solution)/shard_map/ppermute | solution.py:374
  49.7 12.8 %collective-permute-start.19 = (bf16[2,128,512]{2,1,0:T(8,128)(2,1)S(1)}, bf16[2,128,512]{2,1,0:T(8,128)(2,1)S(1)}, u32[]{:S(2)}, u32[]{:S(2)}) collective-permute-start(bf16[2,128,512]{2,1,0:T(8,128)(2,1)S(1)} %get-tuple-element.78), channel_id=1, source_target_pairs={{0,4},{2,6},{4,0},{6,2},{1,5},{3,7},{5,1},{7,3},{8,12},{10,14},{12... | collective-permute-start | bytes 786440 | tf_op jit(solution)/shard_map/ppermute | solution.py:374
  62.5 5.1 %collective-permute-start.20 = (bf16[128,512]{1,0:T(8,128)(2,1)S(1)}, bf16[128,512]{1,0:T(8,128)(2,1)S(1)}, u32[]{:S(2)}, u32[]{:S(2)}) collective-permute-start(bf16[128,512]{1,0:T(8,128)(2,1)S(1)} %get-tuple-element.80), channel_id=1, source_target_pairs={{0,1},{1,0},{2,3},{3,2},{4,5},{5,4},{6,7},{7,6},{8,9},{9,8},{10,11... | collective-permute-start | bytes 393224 | tf_op jit(solution)/shard_map/ppermute | solution.py:373
  63.6 7.1 %collective-permute-start.14 = (bf16[128,512]{1,0:T(8,128)(2,1)S(1)}, bf16[128,512]{1,0:T(8,128)(2,1)S(1)}, u32[]{:S(2)}, u32[]{:S(2)}) collective-permute-start(bf16[128,512]{1,0:T(8,128)(2,1)S(1)} %get-tuple-element.72), channel_id=1, source_target_pairs={{0,2},{2,4},{4,6},{6,0},{1,3},{3,5},{5,7},{7,1},{8,10},{10,12},{12... | collective-permute-start | bytes 393224 | tf_op jit(solution)/shard_map/ppermute | solution.py:374
  64.8 6.2 %collective-permute-start.15 = (bf16[128,512]{1,0:T(8,128)(2,1)S(1)}, bf16[128,512]{1,0:T(8,128)(2,1)S(1)}, u32[]{:S(2)}, u32[]{:S(2)}) collective-permute-start(bf16[128,512]{1,0:T(8,128)(2,1)S(1)} %get-tuple-element.73), channel_id=1, source_target_pairs={{0,6},{2,0},{4,2},{6,4},{1,7},{3,1},{5,3},{7,5},{8,14},{10,8},{12,... | collective-permute-start | bytes 393224 | tf_op jit(solution)/shard_map/ppermute | solution.py:374
  66.9 6.5 %collective-permute-start.16 = (bf16[128,512]{1,0:T(8,128)(2,1)S(1)}, bf16[128,512]{1,0:T(8,128)(2,1)S(1)}, u32[]{:S(2)}, u32[]{:S(2)}) collective-permute-start(bf16[128,512]{1,0:T(8,128)(2,1)S(1)} %get-tuple-element.74), channel_id=1, source_target_pairs={{0,4},{2,6},{4,0},{6,2},{1,5},{3,7},{5,1},{7,3},{8,12},{10,14},{12... | collective-permute-start | bytes 393224 | tf_op jit(solution)/shard_map/ppermute | solution.py:374

commit v3 on v2

--- a/solution.py
+++ b/solution.py
@@ -8,7 +8,9 @@
 
 HD = 128
 SIDE = 4
-AWAY = (1, 3, 2)
+FAR = 2
+AWAY = (1, 3)
+NEAR = (0, 1, 3)
 LOWEST = -1e30
 LOG2E = 1.4426950408889634
 SCALE = LOG2E * HD ** (-0.5)
@@ -221,16 +223,14 @@
         for h in range(heads):
             att_ref[:, h * HD : (h + 1) * HD] = (live[3][h] * (1.0 / live[2][h])).astype(jnp.bfloat16).T
 
-        def one(d, _):
-            start = column(where_ref, d, 1, width)
-            out_ref[d] = project(att_ref[:first], weight_ref, start, width).astype(jnp.bfloat16)
-            return 0
-
-        lax.fori_loop(0, SIDE, one, 0)
-
-    return pl.pallas_call(
-        kernel,
-        out_shape=(sds((rows, heads * HD), jnp.bfloat16), sds((SIDE, first, width), jnp.bfloat16)),
+        out_ref[:rows] = project(att_ref[...], weight_ref, column(where_ref, FAR, 1, width), width).astype(jnp.bfloat16)
+        for i, d in enumerate(NEAR):
+            terms = project(att_ref[:first], weight_ref, column(where_ref, d, 1, width), width)
+            out_ref[rows + i * first : rows + (i + 1) * first] = terms.astype(jnp.bfloat16)
+
+    return pl.pallas_call(
+        kernel,
+        out_shape=(sds((rows, heads * HD), jnp.bfloat16), sds((rows + len(NEAR) * first, width), jnp.bfloat16)),
         in_specs=[SMEM] + [VMEM] * 6,
         out_specs=(VMEM,) * 2,
         scratch_shapes=[pltpu.VMEM(a.shape, a.dtype) for a in state[1:]],
@@ -261,21 +261,20 @@
 
 
 def project_here(where, att, out_weight, first, width):
-    rows = att.shape[0] - first
+    full = att.shape[0]
+    rows = full - first
 
     def kernel(where_ref, att_ref, weight_ref, last_ref, first_ref):
         for flip in range(2):
             last_ref[flip] = project(att_ref[first:], weight_ref, column(where_ref, 0, flip, width), width)
-
-        def one(d, _):
-            first_ref[d] = project(att_ref[:first], weight_ref, column(where_ref, d, 0, width), width)
-            return 0
-
-        lax.fori_loop(0, SIDE, one, 0)
-
-    return pl.pallas_call(
-        kernel,
-        out_shape=(sds((2, rows, width), jnp.float32), sds((SIDE, first, width), jnp.float32)),
+        first_ref[:full] = project(att_ref[...], weight_ref, column(where_ref, FAR, 0, width), width)
+        for i, d in enumerate(NEAR):
+            terms = project(att_ref[:first], weight_ref, column(where_ref, d, 0, width), width)
+            first_ref[full + i * first : full + (i + 1) * first] = terms
+
+    return pl.pallas_call(
+        kernel,
+        out_shape=(sds((2, rows, width), jnp.float32), sds((full + len(NEAR) * first, width), jnp.float32)),
         in_specs=[SMEM, VMEM, VMEM],
         out_specs=(VMEM,) * 2,
         compiler_params=params(),
@@ -284,19 +283,22 @@
     )(where, att, out_weight)
 
 
-def add_first(kept, got):
-    _, rows, width = kept.shape
-
-    def kernel(kept_ref, got_ref, here_ref, *outs):
-        here_ref[...] = kept_ref[0] + got_ref[0].astype(jnp.float32)
-        for out_ref, d in zip(outs, AWAY):
-            out_ref[...] = (kept_ref[d] + got_ref[d].astype(jnp.float32)).astype(jnp.bfloat16)
-
-    return pl.pallas_call(
-        kernel,
-        out_shape=(sds((rows, width), jnp.float32),) + (sds((rows, width), jnp.bfloat16),) * len(AWAY),
+def add_first(kept, got, first):
+    total, width = kept.shape
+    full = total - len(NEAR) * first
+
+    def kernel(kept_ref, got_ref, here_ref, far_ref, *outs):
+        far_ref[...] = (kept_ref[:full] + got_ref[:full].astype(jnp.float32)).astype(jnp.bfloat16)
+        for i, out_ref in enumerate((here_ref, *outs)):
+            here = slice(full + i * first, full + (i + 1) * first)
+            out_ref[...] = (kept_ref[here] + got_ref[here].astype(jnp.float32)).astype(out_ref.dtype)
+
+    near = sds((first, width), jnp.bfloat16)
+    return pl.pallas_call(
+        kernel,
+        out_shape=(sds((first, width), jnp.float32), sds((full, width), jnp.bfloat16)) + (near,) * len(AWAY),
         in_specs=[VMEM] * 2,
-        out_specs=(VMEM,) * (1 + len(AWAY)),
+        out_specs=(VMEM,) * (2 + len(AWAY)),
         compiler_params=params(),
         cost_estimate=pl.CostEstimate(flops=kept.size, bytes_accessed=8 * kept.size, transcendentals=0),
         name="add_first",
@@ -322,23 +324,24 @@
     )(kept, *got)
 
 
-def finish(first_here, first_got, last_here, last_got):
+def finish(first_here, first_got, far_got, last_here, last_got):
     rows, width = first_here.shape
     more = last_here.shape[0]
 
     def kernel(first_ref, *refs):
-        *got_refs, last_ref, swapped_ref, out_ref = refs
-        out_ref[:rows] = (first_ref[...] + sum(r[...].astype(jnp.float32) for r in got_refs)).astype(jnp.bfloat16)
-        out_ref[rows:] = (last_ref[...] + swapped_ref[...].astype(jnp.float32)).astype(jnp.bfloat16)
+        *got_refs, far_ref, last_ref, swapped_ref, out_ref = refs
+        far = far_ref[...].astype(jnp.float32)
+        out_ref[:rows] = (first_ref[...] + far[:rows] + sum(r[...].astype(jnp.float32) for r in got_refs)).astype(jnp.bfloat16)
+        out_ref[rows:] = (last_ref[...] + far[rows:] + swapped_ref[...].astype(jnp.float32)).astype(jnp.bfloat16)
 
     return pl.pallas_call(
         kernel,
         out_shape=sds((rows + more, width), jnp.bfloat16),
-        in_specs=[VMEM] * (3 + len(first_got)),
+        in_specs=[VMEM] * (4 + len(first_got)),
         out_specs=VMEM,
         compiler_params=params(),
         name="finish",
-    )(first_here, *first_got, last_here, last_got)
+    )(first_here, *first_got, far_got, last_here, last_got)
 
 
 def steps(queries, keys, values, out_weight):
@@ -368,7 +371,7 @@
     last = swap(ahead[half])
     mine = join(where, state, parted, stats, ahead[half], half)
     width = out_weight.shape[1] // (2 * SIDE)
-    first = queries.shape[0] // 2
+    first = queries.shape[0] * 4 // 16
     att, send = close(where, (state[0], *mine), last, half, out_weight, first, width)
     across = lambda a: lax.ppermute(a, "x", [(0, 1), (1, 0)])
     along = lambda a, d: lax.ppermute(a, "y", [(i, (i + d) % SIDE) for i in range(SIDE)])
@@ -376,11 +379,12 @@
     away = project_away(where, att, out_weight, first, width)
     got_y = [along(a, d) for a, d in zip(away, AWAY)]
     last_kept, first_kept = project_here(where, att, out_weight, first, width)
-    first_here, *first_away = add_first(first_kept, got_x)
+    first_here, far_away, *first_away = add_first(first_kept, got_x, first)
+    far_got = along(far_away, FAR)
     first_got = [along(a, d) for a, d in zip(first_away, AWAY)]
     last_here, last_away = add_last(last_kept, got_y)
     last_got = across(last_away)
-    return finish(first_here, first_got, last_here, last_got)
+    return finish(first_here, first_got, far_got, last_here, last_got)
 
 
 def solution(mesh):

time: 74.3 us -> 67.5 us (0.908)
  the two profiles are of different devices: /device:TPU:132 before, /device:TPU:128 now
where the time goes in v3:
time: 67.5 us; the launch traced here: 67.3 us
  starting transfers between devices  24.3 us (36%)
  Pallas kernels  20.7 us (31%)
  waiting for transfers between devices  20 us (30%)
  local copies, waits for them, and re-layouts  1.14 us (2%)
  other arithmetic  0.89 us (1%)
    ppermute x4, waiting for transfers between devices, steps(): ahead.append(lax.ppermute(ahead[-1], 'z', up))  13.3 us
    ppermute x5, starting transfers between devices, steps(): lax.ppermute(a, 'y', [(i, (i + d) % SIDE) for i in range(SIDE)])  10 us
    pallas_call x4, Pallas kernels, fold(): pl.pallas_call(kernel, out_shape=tuple((sds(a.shape, a.dtype) for a in st...  9.48 us
    ppermute x3, starting transfers between devices, steps(): behind.append(lax.ppermute(behind[-1], 'z', down))  8.68 us
    ppermute x2, waiting for transfers between devices, steps(): across = lambda a: lax.ppermute(a, 'x', [(0, 1), (1, 0)])  3.93 us
    ppermute x2, starting transfers between devices, steps(): across = lambda a: lax.ppermute(a, 'x', [(0, 1), (1, 0)])  3.13 us
    ppermute x5, waiting for transfers between devices, steps(): lax.ppermute(a, 'y', [(i, (i + d) % SIDE) for i in range(SIDE)])  2.83 us
    pallas_call x1, Pallas kernels, close(): pl.pallas_call(kernel, out_shape=(sds((rows, heads * HD), jnp.bfloat16),...  2.63 us
  transfers between devices with their start and end apart: 20, of which 5 were waited for; matrix products, arithmetic and copies ran while one was open for 1% of the time, Pallas kernels for 21%

profile of v3, /device:TPU:128, one launch (start us, length us, event | category | flops | bytes accessed | tf_op | source)
XLA Modules:
  0.0 67.3 jit_solution(7402986716539321156)
XLA Ops:
  0.9 1.1 %collective-permute-start = (bf16[2,256,128]{2,1,0:T(8,128)(2,1)S(1)}, bf16[2,256,128]{2,1,0:T(8,128)(2,1)S(1)}, u32[]{:S(2)}, u32[]{:S(2)}) collective-permute-start(bf16[2,256,128]{2,1,0:T(8,128)(2,1)S(1)} %pad_maximum_fusion.own_ref), channel_id=1, source_target_pairs={{0,16},{16,32},{32,48},{48,64},{64,80},{80,96},{96,112},{112,0},{1... | collective-permute-start | bytes 393224 | tf_op jit(solution)/shard_map/ppermute | solution.py:359
  2.0 2.2 %collective-permute-start.6 = (bf16[2,256,128]{2,1,0:T(8,128)(2,1)S(1)}, bf16[2,256,128]{2,1,0:T(8,128)(2,1)S(1)}, u32[]{:S(2)}, u32[]{:S(2)}) collective-permute-start(bf16[2,256,128]{2,1,0:T(8,128)(2,1)S(1)} %pad_maximum_fusion.own_ref), channel_id=1, source_target_pairs={{0,112},{16,0},{32,16},{48,32},{64,48},{80,64},{96,80},{112,96},{1... | collective-permute-start | bytes 393224 | tf_op jit(solution)/shard_map/ppermute | solution.py:361
  4.3 3.8 %collective-permute-done.ahead_ref = bf16[2,256,128]{2,1,0:T(8,128)(2,1)S(1)} collective-permute-done((bf16[2,256,128]{2,1,0:T(8,128)(2,1)S(1)}, bf16[2,256,128]{2,1,0:T(8,128)(2,1)S(1)}, u32[]{:S(2)}, u32[]{:S(2)}) %collective-permute-start) | collective-permute-done | bytes 131104 | tf_op jit(solution)/shard_map/ppermute | solution.py:359
  8.1 3.2 %collective-permute-start.7 = (bf16[2,256,128]{2,1,0:T(8,128)(2,1)S(1)}, bf16[2,256,128]{2,1,0:T(8,128)(2,1)S(1)}, u32[]{:S(2)}, u32[]{:S(2)}) collective-permute-start(bf16[2,256,128]{2,1,0:T(8,128)(2,1)S(1)} %collective-permute-done.6.behind_ref), channel_id=1, source_target_pairs={{0,112},{16,0},{32,16},{48,32},{64,48},{80,64},{96,80},{112,96},{1... | collective-permute-start | bytes 393224 | tf_op jit(solution)/shard_map/ppermute | solution.py:361
  12.4 2.4 %open_state.1 = (bf16[16,128,256]{2,1,0:T(8,128)(2,1)S(1)}, f32[16,1,256]{2,1,0:T(1,128)S(1)}, f32[16,1,256]{2,1,0:T(1,128)S(1)}, f32[16,128,256]{2,1,0:T(8,128)S(1)}) custom-call(s32[5]{0:T(128)S(1)} %stack.28.where_ref, bf16[256,1024]{1,0:T(8,128)(2,1)S(1)} %copy-done, bf16[256,1024]{1,0:T(8,128)(2,1)S(1)} %collective-permute-done.10.others_ref, ...), custom_call_target="tpu_custom_call" | custom-call | flops 536870912 | bytes 2228224 | tf_op jit(solution)/shard_map/open_state/pallas_call | solution.py:113
  14.8 3.0 %shard_map.46 = (bf16[16,128,256]{2,1,0:T(8,128)(2,1)S(1)}, f32[16,1,256]{2,1,0:T(1,128)S(1)}, f32[16,1,256]{2,1,0:T(1,128)S(1)}, f32[16,128,256]{2,1,0:T(8,128)S(1)}) custom-call(s32[5]{0:T(128)S(1)} %stack.28.where_ref, ...), custom_call_target="tpu_custom_call", output_to_operand_aliasing={{0}: (3, {}), {1}: (4, {}), {2}: (5, {}), {3}: (6, {})} | custom-call | flops 1073741824 | bytes 2359296 | tf_op jit(solution)/shard_map/pallas_call | solution.py:159
  17.8 3.0 %shard_map.47 = (bf16[16,128,256]{2,1,0:T(8,128)(2,1)S(1)}, f32[16,1,256]{2,1,0:T(1,128)S(1)}, f32[16,1,256]{2,1,0:T(1,128)S(1)}, f32[16,128,256]{2,1,0:T(8,128)...) custom-call(s32[5]{0:T(128)S(1)} %stack.28.where_ref, ...), custom_call_target="tpu_custom_call", output_to_operand_aliasing={{0}: (3, {}), {1}: (4, {}), {2}: (5, {}), {3}: (6, {})} | custom-call | flops 1073741824 | bytes 2359296 | tf_op jit(solution)/shard_map/pallas_call | solution.py:159
  21.2 3.2 %collective-permute-start.8 = (bf16[2,256,128]{2,1,0:T(8,128)(2,1)S(1)}, bf16[2,256,128]{2,1,0:T(8,128)(2,1)S(1)}, u32[]{:S(2)}, u32[]{:S(2)}) collective-permute-start(bf16[2,256,128]{2,1,0:T(8,128)(2,1)S(1)} %collective-permute-done.7.behind_ref), channel_id=1, source_target_pairs={{0,112},{16,0},{32,16},{48,32},{64,48},{80,64},{96,80},{112,96},{1... | collective-permute-start | bytes 393224 | tf_op jit(solution)/shard_map/ppermute | solution.py:361
  24.4 3.8 %collective-permute-done.2.ahead_ref = bf16[2,256,128]{2,1,0:T(8,128)(2,1)S(1)} collective-permute-done((bf16[2,256,128]{2,1,0:T(8,128)(2,1)S(1)}, bf16[2,256,128]{2,1,0:T(8,128)(2,1)S(1)}, u32[]{:S(2)}, u32[]{:S(2)}) %collective-permute-start.2) | collective-permute-done | bytes 131104 | tf_op jit(solution)/shard_map/ppermute | solution.py:359
  28.7 5.7 %collective-permute-done.3.ahead_ref = bf16[2,256,128]{2,1,0:T(8,128)(2,1)S(1)} collective-permute-done((bf16[2,256,128]{2,1,0:T(8,128)(2,1)S(1)}, bf16[2,256,128]{2,1,0:T(8,128)(2,1)S(1)}, u32[]{:S(2)}, u32[]{:S(2)}) %collective-permute-start.3) | collective-permute-done | bytes 131104 | tf_op jit(solution)/shard_map/ppermute | solution.py:359
  34.9 1.7 %shard_map.48 = (bf16[16,128,256]{2,1,0:T(8,128)(2,1)S(1)}, f32[16,1,256]{2,1,0:T(1,128)S(1)}, f32[16,1,256]{2,1,0:T(1,128)S(1)}, f32[16,128,256]{2,1,0:T(8,128)S(1)}) custom-call(s32[5]{0:T(128)S(1)} %stack.28.where_ref, ...), custom_call_target="tpu_custom_call", output_to_operand_aliasing={{0}: (3, {}), {1}: (4, {}), {2}: (5, {}), {3}: (6, {})} | custom-call | flops 536870912 | bytes 1310720 | tf_op jit(solution)/shard_map/pallas_call | solution.py:159
  36.7 1.8 %shard_map.49 = (bf16[16,128,256]{2,1,0:T(8,128)(2,1)S(1)}, f32[16,1,256]{2,1,0:T(1,128)S(1)}, f32[16,1,256]{2,1,0:T(1,128)S(1)}, f32[16,128,256]{2,1,0:T(8,128)S(1)}) custom-call(s32[5]{0:T(128)S(1)} %stack.28.where_ref, ...), custom_call_target="tpu_custom_call", output_to_operand_aliasing={{0}: (3, {}), {1}: (4, {}), {2}: (5, {}), {3}: (6, {})} | custom-call | flops 536870912 | bytes 1310720 | tf_op jit(solution)/shard_map/pallas_call | solution.py:159
  38.5 1.7 %join.1 = (f32[8,1,256]{2,1,0:T(1,128)S(1)}, f32[8,1,256]{2,1,0:T(1,128)S(1)}, f32[8,128,256]{2,1,0:T(8,128)S(1)}) custom-call(s32[5]{0:T(128)S(1)} %stack.28.where_ref, bf16[8,128,256]{2,1,0:T(8,128)(2,1)S(1)} %collective-permute-done.11.parted_ref, f32[2,8,1,256]{3,2,1,0:T(1,128)S(1)} %collective-permute-done.12.stats_ref, ...), custom_call_target="tpu_custom_call" | custom-call | flops 268435456 | bytes 1179648 | tf_op jit(solution)/shard_map/join/pallas_call | solution.py:190
  40.2 2.6 %close.1 = (bf16[256,1024]{1,0:T(8,128)(2,1)S(1)}, bf16[448,512]{1,0:T(8,128)(2,1)S(1)}) custom-call(s32[5]{0:T(128)S(1)} %stack.28.where_ref, bf16[2,256,128]{2,1,0:T(8,128)(2,1)S(1)} %collective-permute-done.4.ahead_ref, bf16[16,128,256]{2,1,0:T(8,128)(2,1)S(1)} %get-tuple-element.58.refs_0_.q_ref, f32[8,1,256]{2,1,0:T(1,128)S(1)} %get-tuple-element.64.top_ref, ...), custom_call_target="tpu_custom_call" | custom-call | flops 536870912 | bytes 1310720 | tf_op jit(solution)/shard_map/close/pallas_call | solution.py:231
  42.8 1.6 %collective-permute-start.13 = (bf16[448,512]{1,0:T(8,128)(2,1)S(1)}, bf16[448,512]{1,0:T(8,128)(2,1)S(1)}, u32[]{:S(2)}, u32[]{:S(2)}) collective-permute-start(bf16[448,512]{1,0:T(8,128)(2,1)S(1)} %get-tuple-element.69), channel_id=1, source_target_pairs={{0,1},{1,0},{2,3},{3,2},{4,5},{5,4},{6,7},{7,6},{8,9},{9,8},{10,11... | collective-permute-start | bytes 1376264 | tf_op jit(solution)/shard_map/ppermute | solution.py:376
  44.4 1.6 %project_away.1 = (bf16[2,192,512]{2,1,0:T(8,128)(2,1)S(1)}, bf16[2,192,512]{2,1,0:T(8,128)(2,1)S(1)}) custom-call(s32[5]{0:T(128)S(1)} %stack.28.where_ref, bf16[256,1024]{1,0:T(8,128)(2,1)S(1)} %get-tuple-element.67.att_ref, bf16[1024,4096]{1,0:T(8,128)(2,1)S(1)} %bitcast.7), custom_call_target="tpu_custom_call" | custom-call | flops 301989888 | bytes 983040 | tf_op jit(solution)/shard_map/project_away/pallas_call | solution.py:252
  46.0 1.9 %collective-permute-start.17 = (bf16[2,192,512]{2,1,0:T(8,128)(2,1)S(1)}, bf16[2,192,512]{2,1,0:T(8,128)(2,1)S(1)}, u32[]{:S(2)}, u32[]{:S(2)}) collective-permute-start(bf16[2,192,512]{2,1,0:T(8,128)(2,1)S(1)} %get-tuple-element.75), channel_id=1, source_target_pairs={{0,2},{2,4},{4,6},{6,0},{1,3},{3,5},{5,7},{7,1},{8,10},{10,12},{12... | collective-permute-start | bytes 1179656 | tf_op jit(solution)/shard_map/ppermute | solution.py:377
  47.8 1.7 %collective-permute-start.18 = (bf16[2,192,512]{2,1,0:T(8,128)(2,1)S(1)}, bf16[2,192,512]{2,1,0:T(8,128)(2,1)S(1)}, u32[]{:S(2)}, u32[]{:S(2)}) collective-permute-start(bf16[2,192,512]{2,1,0:T(8,128)(2,1)S(1)} %get-tuple-element.76), channel_id=1, source_target_pairs={{0,6},{2,0},{4,2},{6,4},{1,7},{3,1},{5,3},{7,5},{8,14},{10,8},{12,... | collective-permute-start | bytes 1179656 | tf_op jit(solution)/shard_map/ppermute | solution.py:377
  49.5 1.9 %project_here.1 = (f32[2,192,512]{2,1,0:T(8,128)S(1)}, f32[448,512]{1,0:T(8,128)S(1)}) custom-call(s32[5]{0:T(128)S(1)} %stack.28.where_ref, bf16[256,1024]{1,0:T(8,128)(2,1)S(1)} %get-tuple-element.67.att_ref, bf16[1024,4096]{1,0:T(8,128)(2,1)S(1)} %bitcast.7), custom_call_target="tpu_custom_call" | custom-call | flops 301989888 | bytes 983040 | tf_op jit(solution)/shard_map/project_here/pallas_call | solution.py:275
  51.4 3.9 %collective-permute-done.13.got_ref = bf16[448,512]{1,0:T(8,128)(2,1)S(1)} collective-permute-done((bf16[448,512]{1,0:T(8,128)(2,1)S(1)}, bf16[448,512]{1,0:T(8,128)(2,1)S(1)}, u32[]{:S(2)}, u32[]{:S(2)}) %collective-permute-start.13) | collective-permute-done | bytes 458784 | tf_op jit(solution)/shard_map/ppermute | solution.py:376
  55.4 3.3 %collective-permute-start.16 = (bf16[256,512]{1,0:T(8,128)(2,1)S(1)}, bf16[256,512]{1,0:T(8,128)(2,1)S(1)}, u32[]{:S(2)}, u32[]{:S(2)}) collective-permute-start(bf16[256,512]{1,0:T(8,128)(2,1)S(1)} %get-tuple-element.73), channel_id=1, source_target_pairs={{0,4},{2,6},{4,0},{6,2},{1,5},{3,7},{5,1},{7,3},{8,12},{10,14},{12... | collective-permute-start | bytes 786440 | tf_op jit(solution)/shard_map/ppermute | solution.py:377
  58.8 1.6 %collective-permute-start.19 = (bf16[192,512]{1,0:T(8,128)(2,1)S(1)}, bf16[192,512]{1,0:T(8,128)(2,1)S(1)}, u32[]{:S(2)}, u32[]{:S(2)}) collective-permute-start(bf16[192,512]{1,0:T(8,128)(2,1)S(1)} %get-tuple-element.78), channel_id=1, source_target_pairs={{0,1},{1,0},{2,3},{3,2},{4,5},{5,4},{6,7},{7,6},{8,9},{9,8},{10,11... | collective-permute-start | bytes 589832 | tf_op jit(solution)/shard_map/ppermute | solution.py:376
  61.1 2.6 %collective-permute-start.15 = (bf16[64,512]{1,0:T(8,128)(2,1)S(1)}, bf16[64,512]{1,0:T(8,128)(2,1)S(1)}, u32[]{:S(2)}, u32[]{:S(2)}) collective-permute-start(bf16[64,512]{1,0:T(8,128)(2,1)S(1)} %get-tuple-element.72), channel_id=1, source_target_pairs={{0,6},{2,0},{4,2},{6,4},{1,7},{3,1},{5,3},{7,5},{8,14},{10,8},{12,... | collective-permute-start | bytes 196616 | tf_op jit(solution)/shard_map/ppermute | solution.py:377
  63.6 2.8 %collective-permute-done.14.refs_0_ = bf16[64,512]{1,0:T(8,128)(2,1)S(1)} collective-permute-done((bf16[64,512]{1,0:T(8,128)(2,1)S(1)}, bf16[64,512]{1,0:T(8,128)(2,1)S(1)}, u32[]{:S(2)}, u32[]{:S(2)}) %collective-permute-start.14) | collective-permute-done | bytes 65568 | tf_op jit(solution)/shard_map/ppermute | solution.py:377
  (37 shorter events, 5.1 us)
Async XLA Ops:
  0.0 11.3 %collective-permute-start.10 = (bf16[256,1024]{1,0:T(8,128)(2,1)}, bf16[256,1024]{1,0:T(8,128)(2,1)S(1)}, u32[]{:S(2)}, u32[]{:S(2)}) collective-permute-start(bf16[256,1024]{1,0:T(8,128)(2,1)} %queries_ref.1), channel_id=1, source_target_pairs={{0,8},{8,0},{1,9},{9,1},{2,10},{10,2},{3,11},{11,3},{4,12},{12,4},... | collective-permute-start | bytes 1572872 | tf_op jit(solution)/shard_map/ppermute | solution.py:352
  0.9 7.2 %collective-permute-start = (bf16[2,256,128]{2,1,0:T(8,128)(2,1)S(1)}, bf16[2,256,128]{2,1,0:T(8,128)(2,1)S(1)}, u32[]{:S(2)}, u32[]{:S(2)}) collective-permute-start(bf16[2,256,128]{2,1,0:T(8,128)(2,1)S(1)} %pad_maximum_fusion.own_ref), channel_id=1, source_target_pairs={{0,16},{16,32},{32,48},{48,64},{64,80},{80,96},{96,112},{112,0},{1... | collective-permute-start | bytes 393224 | tf_op jit(solution)/shard_map/ppermute | solution.py:359
  2.0 6.1 %collective-permute-start.6 = (bf16[2,256,128]{2,1,0:T(8,128)(2,1)S(1)}, bf16[2,256,128]{2,1,0:T(8,128)(2,1)S(1)}, u32[]{:S(2)}, u32[]{:S(2)}) collective-permute-start(bf16[2,256,128]{2,1,0:T(8,128)(2,1)S(1)} %pad_maximum_fusion.own_ref), channel_id=1, source_target_pairs={{0,112},{16,0},{32,16},{48,32},{64,48},{80,64},{96,80},{112,96},{1... | collective-permute-start | bytes 393224 | tf_op jit(solution)/shard_map/ppermute | solution.py:361
  8.1 9.7 %collective-permute-start.1 = (bf16[2,256,128]{2,1,0:T(8,128)(2,1)S(1)}, bf16[2,256,128]{2,1,0:T(8,128)(2,1)S(1)}, u32[]{:S(2)}, u32[]{:S(2)}) collective-permute-start(bf16[2,256,128]{2,1,0:T(8,128)(2,1)S(1)} %collective-permute-done.ahead_ref), channel_id=1, source_target_pairs={{0,16},{16,32},{32,48},{48,64},{64,80},{80,96},{96,112},{112,0},{1... | collective-permute-start | bytes 393224 | tf_op jit(solution)/shard_map/ppermute | solution.py:359
  8.1 9.7 %collective-permute-start.7 = (bf16[2,256,128]{2,1,0:T(8,128)(2,1)S(1)}, bf16[2,256,128]{2,1,0:T(8,128)(2,1)S(1)}, u32[]{:S(2)}, u32[]{:S(2)}) collective-permute-start(bf16[2,256,128]{2,1,0:T(8,128)(2,1)S(1)} %collective-permute-done.6.behind_ref), channel_id=1, source_target_pairs={{0,112},{16,0},{32,16},{48,32},{64,48},{80,64},{96,80},{112,96},{1... | collective-permute-start | bytes 393224 | tf_op jit(solution)/shard_map/ppermute | solution.py:361
  11.3 1.0 %copy-start = (bf16[256,1024]{1,0:T(8,128)(2,1)S(1)}, bf16[256,1024]{1,0:T(8,128)(2,1)}, u32[]{:S(2)}) copy-start(bf16[256,1024]{1,0:T(8,128)(2,1)} %queries_ref.1) | copy-start | bytes 1572868
  14.8 25.4 %slice-start = ((s8[8388608]{0:T(1024)(128)(4,1)}), s8[4194304]{0:T(1024)(128)(4,1)S(1)}, s32[]{:S(2)}) async-start(s8[8388608]{0:T(1024)(128)(4,1)} %bitcast.6), calls=%async_computation | async-start | bytes 8388608
  20.8 17.6 %collective-permute-start.11 = (bf16[8,128,256]{2,1,0:T(8,128)(2,1)S(1)}, bf16[8,128,256]{2,1,0:T(8,128)(2,1)S(1)}, u32[]{:S(2)}, u32[]{:S(2)}) collective-permute-start(bf16[8,128,256]{2,1,0:T(8,128)(2,1)S(1)} %get-tuple-element.59), channel_id=1, source_target_pairs={{0,8},{8,0},{1,9},{9,1},{2,10},{10,2},{3,11},{11,3},{4,12},{12,4},... | collective-permute-start | bytes 1572872 | tf_op jit(solution)/shard_map/ppermute | solution.py:352
  21.1 7.1 %collective-permute-start.2 = (bf16[2,256,128]{2,1,0:T(8,128)(2,1)S(1)}, bf16[2,256,128]{2,1,0:T(8,128)(2,1)S(1)}, u32[]{:S(2)}, u32[]{:S(2)}) collective-permute-start(bf16[2,256,128]{2,1,0:T(8,128)(2,1)S(1)} %collective-permute-done.1.ahead_ref), channel_id=1, source_target_pairs={{0,16},{16,32},{32,48},{48,64},{64,80},{80,96},{96,112},{112,0},{1... | collective-permute-start | bytes 393224 | tf_op jit(solution)/shard_map/ppermute | solution.py:359
  21.2 7.0 %collective-permute-start.8 = (bf16[2,256,128]{2,1,0:T(8,128)(2,1)S(1)}, bf16[2,256,128]{2,1,0:T(8,128)(2,1)S(1)}, u32[]{:S(2)}, u32[]{:S(2)}) collective-permute-start(bf16[2,256,128]{2,1,0:T(8,128)(2,1)S(1)} %collective-permute-done.7.behind_ref), channel_id=1, source_target_pairs={{0,112},{16,0},{32,16},{48,32},{64,48},{80,64},{96,80},{112,96},{1... | collective-permute-start | bytes 393224 | tf_op jit(solution)/shard_map/ppermute | solution.py:361
  28.2 6.2 %collective-permute-start.3 = (bf16[2,256,128]{2,1,0:T(8,128)(2,1)S(1)}, bf16[2,256,128]{2,1,0:T(8,128)(2,1)S(1)}, u32[]{:S(2)}, u32[]{:S(2)}) collective-permute-start(bf16[2,256,128]{2,1,0:T(8,128)(2,1)S(1)} %collective-permute-done.2.ahead_ref), channel_id=1, source_target_pairs={{0,16},{16,32},{32,48},{48,64},{64,80},{80,96},{96,112},{112,0},{1... | collective-permute-start | bytes 393224 | tf_op jit(solution)/shard_map/ppermute | solution.py:359
  28.2 8.4 %collective-permute-start.5 = (bf16[2,256,128]{2,1,0:T(8,128)(2,1)S(1)}, bf16[2,256,128]{2,1,0:T(8,128)(2,1)S(1)}, u32[]{:S(2)}, u32[]{:S(2)}) collective-permute-start(bf16[2,256,128]{2,1,0:T(8,128)(2,1)S(1)} %collective-permute-done.2.ahead_ref), channel_id=1, source_target_pairs={{0,8},{8,0},{1,9},{9,1},{2,10},{10,2},{3,11},{11,3},{4,12},{12,4},... | collective-permute-start | bytes 393224 | tf_op jit(solution)/shard_map/ppermute | solution.py:352
  28.2 8.4 %collective-permute-start.9 = (bf16[2,256,128]{2,1,0:T(8,128)(2,1)S(1)}, bf16[2,256,128]{2,1,0:T(8,128)(2,1)S(1)}, u32[]{:S(2)}, u32[]{:S(2)}) collective-permute-start(bf16[2,256,128]{2,1,0:T(8,128)(2,1)S(1)} %collective-permute-done.8.behind_ref), channel_id=1, source_target_pairs={{0,8},{8,0},{1,9},{9,1},{2,10},{10,2},{3,11},{11,3},{4,12},{12,4},... | collective-permute-start | bytes 393224 | tf_op jit(solution)/shard_map/ppermute | solution.py:352
  34.4 5.8 %collective-permute-start.4 = (bf16[2,256,128]{2,1,0:T(8,128)(2,1)S(1)}, bf16[2,256,128]{2,1,0:T(8,128)(2,1)S(1)}, u32[]{:S(2)}, u32[]{:S(2)}) collective-permute-start(bf16[2,256,128]{2,1,0:T(8,128)(2,1)S(1)} %collective-permute-done.3.ahead_ref), channel_id=1, source_target_pairs={{0,8},{8,0},{1,9},{9,1},{2,10},{10,2},{3,11},{11,3},{4,12},{12,4},... | collective-permute-start | bytes 393224 | tf_op jit(solution)/shard_map/ppermute | solution.py:352
  34.4 4.0 %collective-permute-start.12 = (f32[2,8,1,256]{3,2,1,0:T(1,128)S(1)}, f32[2,8,1,256]{3,2,1,0:T(1,128)S(1)}, u32[]{:S(2)}, u32[]{:S(2)}) collective-permute-start(f32[2,8,1,256]{3,2,1,0:T(1,128)S(1)} %get-tuple-element.60), channel_id=1, source_target_pairs={{0,8},{8,0},{1,9},{9,1},{2,10},{10,2},{3,11},{11,3},{4,12},{12,4},... | collective-permute-start | bytes 49160 | tf_op jit(solution)/shard_map/ppermute | solution.py:352
  34.9 5.3 %slice-start.1 = ((s8[8388608]{0:T(1024)(128)(4,1)}), s8[4194304]{0:T(1024)(128)(4,1)S(1)}, s32[]{:S(2)}) async-start(s8[8388608]{0:T(1024)(128)(4,1)} %bitcast.6), calls=%async_computation.1 | async-start | bytes 8388608
  42.8 12.5 %collective-permute-start.13 = (bf16[448,512]{1,0:T(8,128)(2,1)S(1)}, bf16[448,512]{1,0:T(8,128)(2,1)S(1)}, u32[]{:S(2)}, u32[]{:S(2)}) collective-permute-start(bf16[448,512]{1,0:T(8,128)(2,1)S(1)} %get-tuple-element.69), channel_id=1, source_target_pairs={{0,1},{1,0},{2,3},{3,2},{4,5},{5,4},{6,7},{7,6},{8,9},{9,8},{10,11... | collective-permute-start | bytes 1376264 | tf_op jit(solution)/shard_map/ppermute | solution.py:376
  46.0 12.7 %collective-permute-start.17 = (bf16[2,192,512]{2,1,0:T(8,128)(2,1)S(1)}, bf16[2,192,512]{2,1,0:T(8,128)(2,1)S(1)}, u32[]{:S(2)}, u32[]{:S(2)}) collective-permute-start(bf16[2,192,512]{2,1,0:T(8,128)(2,1)S(1)} %get-tuple-element.75), channel_id=1, source_target_pairs={{0,2},{2,4},{4,6},{6,0},{1,3},{3,5},{5,7},{7,1},{8,10},{10,12},{12... | collective-permute-start | bytes 1179656 | tf_op jit(solution)/shard_map/ppermute | solution.py:377
  47.8 10.9 %collective-permute-start.18 = (bf16[2,192,512]{2,1,0:T(8,128)(2,1)S(1)}, bf16[2,192,512]{2,1,0:T(8,128)(2,1)S(1)}, u32[]{:S(2)}, u32[]{:S(2)}) collective-permute-start(bf16[2,192,512]{2,1,0:T(8,128)(2,1)S(1)} %get-tuple-element.76), channel_id=1, source_target_pairs={{0,6},{2,0},{4,2},{6,4},{1,7},{3,1},{5,3},{7,5},{8,14},{10,8},{12,... | collective-permute-start | bytes 1179656 | tf_op jit(solution)/shard_map/ppermute | solution.py:377
  55.4 11.1 %collective-permute-start.16 = (bf16[256,512]{1,0:T(8,128)(2,1)S(1)}, bf16[256,512]{1,0:T(8,128)(2,1)S(1)}, u32[]{:S(2)}, u32[]{:S(2)}) collective-permute-start(bf16[256,512]{1,0:T(8,128)(2,1)S(1)} %get-tuple-element.73), channel_id=1, source_target_pairs={{0,4},{2,6},{4,0},{6,2},{1,5},{3,7},{5,1},{7,3},{8,12},{10,14},{12... | collective-permute-start | bytes 786440 | tf_op jit(solution)/shard_map/ppermute | solution.py:377
  58.8 7.6 %collective-permute-start.19 = (bf16[192,512]{1,0:T(8,128)(2,1)S(1)}, bf16[192,512]{1,0:T(8,128)(2,1)S(1)}, u32[]{:S(2)}, u32[]{:S(2)}) collective-permute-start(bf16[192,512]{1,0:T(8,128)(2,1)S(1)} %get-tuple-element.78), channel_id=1, source_target_pairs={{0,1},{1,0},{2,3},{3,2},{4,5},{5,4},{6,7},{7,6},{8,9},{9,8},{10,11... | collective-permute-start | bytes 589832 | tf_op jit(solution)/shard_map/ppermute | solution.py:376
  60.4 6.1 %collective-permute-start.14 = (bf16[64,512]{1,0:T(8,128)(2,1)S(1)}, bf16[64,512]{1,0:T(8,128)(2,1)S(1)}, u32[]{:S(2)}, u32[]{:S(2)}) collective-permute-start(bf16[64,512]{1,0:T(8,128)(2,1)S(1)} %get-tuple-element.71), channel_id=1, source_target_pairs={{0,2},{2,4},{4,6},{6,0},{1,3},{3,5},{5,7},{7,1},{8,10},{10,12},{12... | collective-permute-start | bytes 196616 | tf_op jit(solution)/shard_map/ppermute | solution.py:377
  61.1 5.4 %collective-permute-start.15 = (bf16[64,512]{1,0:T(8,128)(2,1)S(1)}, bf16[64,512]{1,0:T(8,128)(2,1)S(1)}, u32[]{:S(2)}, u32[]{:S(2)}) collective-permute-start(bf16[64,512]{1,0:T(8,128)(2,1)S(1)} %get-tuple-element.72), channel_id=1, source_target_pairs={{0,6},{2,0},{4,2},{6,4},{1,7},{3,1},{5,3},{7,5},{8,14},{10,8},{12,... | collective-permute-start | bytes 196616 | tf_op jit(solution)/shard_map/ppermute | solution.py:377

commit v4 on v3

--- a/solution.py
+++ b/solution.py
@@ -211,10 +211,8 @@
 def close(where, state, ahead, step, out_weight, first, width):
     heads, _, rows = state[3].shape
 
-    def kernel(where_ref, ahead_ref, q_ref, top_ref, sum_ref, acc_ref, weight_ref, att_ref, out_ref, *scratch):
-        live = (q_ref.at[:heads], *scratch)
-        for src, dst in zip((top_ref, sum_ref, acc_ref), live[1:]):
-            dst[...] = src[...]
+    def kernel(where_ref, ahead_ref, q_ref, top_ref, sum_ref, acc_ref, weight_ref, att_ref, out_ref, *_):
+        live = (q_ref.at[:heads], top_ref, sum_ref, acc_ref)
 
         @pl.when(where_ref[0] >= step)
         def _():
@@ -228,16 +226,18 @@
             terms = project(att_ref[:first], weight_ref, column(where_ref, d, 1, width), width)
             out_ref[rows + i * first : rows + (i + 1) * first] = terms.astype(jnp.bfloat16)
 
-    return pl.pallas_call(
-        kernel,
-        out_shape=(sds((rows, heads * HD), jnp.bfloat16), sds((rows + len(NEAR) * first, width), jnp.bfloat16)),
+    att, out, *_ = pl.pallas_call(
+        kernel,
+        out_shape=(sds((rows, heads * HD), jnp.bfloat16), sds((rows + len(NEAR) * first, width), jnp.bfloat16))
+        + tuple(sds(a.shape, a.dtype) for a in state[1:]),
         in_specs=[SMEM] + [VMEM] * 6,
-        out_specs=(VMEM,) * 2,
-        scratch_shapes=[pltpu.VMEM(a.shape, a.dtype) for a in state[1:]],
+        out_specs=(VMEM,) * 5,
+        input_output_aliases={3: 2, 4: 3, 5: 4},
         compiler_params=params(),
         cost_estimate=cost(2 * rows, rows, heads),
         name="close",
     )(where, ahead, *state, out_weight)
+    return att, out
 
 
 def project_away(where, att, out_weight, first, width):

time: 67.5 us -> 67.4 us (level)
  no operation moved by 1% of the time
where the time goes in v4:
time: 67.4 us; the launch traced here: 67.2 us
  starting transfers between devices  24.3 us (36%)
  Pallas kernels  20.6 us (31%)
  waiting for transfers between devices  20.1 us (30%)
  local copies, waits for them, and re-layouts  1.14 us (2%)
  other arithmetic  0.89 us (1%)
    ppermute x4, waiting for transfers between devices, steps(): ahead.append(lax.ppermute(ahead[-1], 'z', up))  13.3 us
    ppermute x5, starting transfers between devices, steps(): lax.ppermute(a, 'y', [(i, (i + d) % SIDE) for i in range(SIDE)])  10 us
    pallas_call x4, Pallas kernels, fold(): pl.pallas_call(kernel, out_shape=tuple((sds(a.shape, a.dtype) for a in st...  9.48 us
    ppermute x3, starting transfers between devices, steps(): behind.append(lax.ppermute(behind[-1], 'z', down))  8.68 us
    ppermute x2, waiting for transfers between devices, steps(): across = lambda a: lax.ppermute(a, 'x', [(0, 1), (1, 0)])  3.95 us
    ppermute x2, starting transfers between devices, steps(): across = lambda a: lax.ppermute(a, 'x', [(0, 1), (1, 0)])  3.09 us
    ppermute x5, waiting for transfers between devices, steps(): lax.ppermute(a, 'y', [(i, (i + d) % SIDE) for i in range(SIDE)])  2.84 us
    pallas_call x1, Pallas kernels, close(): pl.pallas_call(kernel, out_shape=(sds((rows, heads * HD), jnp.bfloat16),...  2.56 us
  transfers between devices with their start and end apart: 20, of which 5 were waited for; matrix products, arithmetic and copies ran while one was open for 1% of the time, Pallas kernels for 21%

profile of v4, /device:TPU:128, one launch (start us, length us, event | category | flops | bytes accessed | tf_op | source)
XLA Modules:
  0.0 67.2 jit_solution(17458183460891469975)
XLA Ops:
  0.9 1.1 %collective-permute-start = (bf16[2,256,128]{2,1,0:T(8,128)(2,1)S(1)}, bf16[2,256,128]{2,1,0:T(8,128)(2,1)S(1)}, u32[]{:S(2)}, u32[]{:S(2)}) collective-permute-start(bf16[2,256,128]{2,1,0:T(8,128)(2,1)S(1)} %pad_maximum_fusion.own_ref), channel_id=1, source_target_pairs={{0,16},{16,32},{32,48},{48,64},{64,80},{80,96},{96,112},{112,0},{1... | collective-permute-start | bytes 393224 | tf_op jit(solution)/shard_map/ppermute | solution.py:359
  2.0 2.2 %collective-permute-start.6 = (bf16[2,256,128]{2,1,0:T(8,128)(2,1)S(1)}, bf16[2,256,128]{2,1,0:T(8,128)(2,1)S(1)}, u32[]{:S(2)}, u32[]{:S(2)}) collective-permute-start(bf16[2,256,128]{2,1,0:T(8,128)(2,1)S(1)} %pad_maximum_fusion.own_ref), channel_id=1, source_target_pairs={{0,112},{16,0},{32,16},{48,32},{64,48},{80,64},{96,80},{112,96},{1... | collective-permute-start | bytes 393224 | tf_op jit(solution)/shard_map/ppermute | solution.py:361
  4.3 3.8 %collective-permute-done.ahead_ref = bf16[2,256,128]{2,1,0:T(8,128)(2,1)S(1)} collective-permute-done((bf16[2,256,128]{2,1,0:T(8,128)(2,1)S(1)}, bf16[2,256,128]{2,1,0:T(8,128)(2,1)S(1)}, u32[]{:S(2)}, u32[]{:S(2)}) %collective-permute-start) | collective-permute-done | bytes 131104 | tf_op jit(solution)/shard_map/ppermute | solution.py:359
  8.1 3.2 %collective-permute-start.7 = (bf16[2,256,128]{2,1,0:T(8,128)(2,1)S(1)}, bf16[2,256,128]{2,1,0:T(8,128)(2,1)S(1)}, u32[]{:S(2)}, u32[]{:S(2)}) collective-permute-start(bf16[2,256,128]{2,1,0:T(8,128)(2,1)S(1)} %collective-permute-done.6.behind_ref), channel_id=1, source_target_pairs={{0,112},{16,0},{32,16},{48,32},{64,48},{80,64},{96,80},{112,96},{1... | collective-permute-start | bytes 393224 | tf_op jit(solution)/shard_map/ppermute | solution.py:361
  12.4 2.4 %open_state.1 = (bf16[16,128,256]{2,1,0:T(8,128)(2,1)S(1)}, f32[16,1,256]{2,1,0:T(1,128)S(1)}, f32[16,1,256]{2,1,0:T(1,128)S(1)}, f32[16,128,256]{2,1,0:T(8,128)S(1)}) custom-call(s32[5]{0:T(128)S(1)} %stack.28.where_ref, bf16[256,1024]{1,0:T(8,128)(2,1)S(1)} %copy-done, bf16[256,1024]{1,0:T(8,128)(2,1)S(1)} %collective-permute-done.10.others_ref, ...), custom_call_target="tpu_custom_call" | custom-call | flops 536870912 | bytes 2228224 | tf_op jit(solution)/shard_map/open_state/pallas_call | solution.py:113
  14.8 3.0 %shard_map.46 = (bf16[16,128,256]{2,1,0:T(8,128)(2,1)S(1)}, f32[16,1,256]{2,1,0:T(1,128)S(1)}, f32[16,1,256]{2,1,0:T(1,128)S(1)}, f32[16,128,256]{2,1,0:T(8,128)S(1)}) custom-call(s32[5]{0:T(128)S(1)} %stack.28.where_ref, ...), custom_call_target="tpu_custom_call", output_to_operand_aliasing={{0}: (3, {}), {1}: (4, {}), {2}: (5, {}), {3}: (6, {})} | custom-call | flops 1073741824 | bytes 2359296 | tf_op jit(solution)/shard_map/pallas_call | solution.py:159
  17.8 3.0 %shard_map.47 = (bf16[16,128,256]{2,1,0:T(8,128)(2,1)S(1)}, f32[16,1,256]{2,1,0:T(1,128)S(1)}, f32[16,1,256]{2,1,0:T(1,128)S(1)}, f32[16,128,256]{2,1,0:T(8,128)...) custom-call(s32[5]{0:T(128)S(1)} %stack.28.where_ref, ...), custom_call_target="tpu_custom_call", output_to_operand_aliasing={{0}: (3, {}), {1}: (4, {}), {2}: (5, {}), {3}: (6, {})} | custom-call | flops 1073741824 | bytes 2359296 | tf_op jit(solution)/shard_map/pallas_call | solution.py:159
  21.2 3.2 %collective-permute-start.8 = (bf16[2,256,128]{2,1,0:T(8,128)(2,1)S(1)}, bf16[2,256,128]{2,1,0:T(8,128)(2,1)S(1)}, u32[]{:S(2)}, u32[]{:S(2)}) collective-permute-start(bf16[2,256,128]{2,1,0:T(8,128)(2,1)S(1)} %collective-permute-done.7.behind_ref), channel_id=1, source_target_pairs={{0,112},{16,0},{32,16},{48,32},{64,48},{80,64},{96,80},{112,96},{1... | collective-permute-start | bytes 393224 | tf_op jit(solution)/shard_map/ppermute | solution.py:361
  24.4 3.8 %collective-permute-done.2.ahead_ref = bf16[2,256,128]{2,1,0:T(8,128)(2,1)S(1)} collective-permute-done((bf16[2,256,128]{2,1,0:T(8,128)(2,1)S(1)}, bf16[2,256,128]{2,1,0:T(8,128)(2,1)S(1)}, u32[]{:S(2)}, u32[]{:S(2)}) %collective-permute-start.2) | collective-permute-done | bytes 131104 | tf_op jit(solution)/shard_map/ppermute | solution.py:359
  28.7 5.7 %collective-permute-done.3.ahead_ref = bf16[2,256,128]{2,1,0:T(8,128)(2,1)S(1)} collective-permute-done((bf16[2,256,128]{2,1,0:T(8,128)(2,1)S(1)}, bf16[2,256,128]{2,1,0:T(8,128)(2,1)S(1)}, u32[]{:S(2)}, u32[]{:S(2)}) %collective-permute-start.3) | collective-permute-done | bytes 131104 | tf_op jit(solution)/shard_map/ppermute | solution.py:359
  34.9 1.7 %shard_map.48 = (bf16[16,128,256]{2,1,0:T(8,128)(2,1)S(1)}, f32[16,1,256]{2,1,0:T(1,128)S(1)}, f32[16,1,256]{2,1,0:T(1,128)S(1)}, f32[16,128,256]{2,1,0:T(8,128)S(1)}) custom-call(s32[5]{0:T(128)S(1)} %stack.28.where_ref, ...), custom_call_target="tpu_custom_call", output_to_operand_aliasing={{0}: (3, {}), {1}: (4, {}), {2}: (5, {}), {3}: (6, {})} | custom-call | flops 536870912 | bytes 1310720 | tf_op jit(solution)/shard_map/pallas_call | solution.py:159
  36.7 1.8 %shard_map.49 = (bf16[16,128,256]{2,1,0:T(8,128)(2,1)S(1)}, f32[16,1,256]{2,1,0:T(1,128)S(1)}, f32[16,1,256]{2,1,0:T(1,128)S(1)}, f32[16,128,256]{2,1,0:T(8,128)S(1)}) custom-call(s32[5]{0:T(128)S(1)} %stack.28.where_ref, ...), custom_call_target="tpu_custom_call", output_to_operand_aliasing={{0}: (3, {}), {1}: (4, {}), {2}: (5, {}), {3}: (6, {})} | custom-call | flops 536870912 | bytes 1310720 | tf_op jit(solution)/shard_map/pallas_call | solution.py:159
  38.5 1.7 %join.1 = (f32[8,1,256]{2,1,0:T(1,128)S(1)}, f32[8,1,256]{2,1,0:T(1,128)S(1)}, f32[8,128,256]{2,1,0:T(8,128)S(1)}) custom-call(s32[5]{0:T(128)S(1)} %stack.28.where_ref, bf16[8,128,256]{2,1,0:T(8,128)(2,1)S(1)} %collective-permute-done.11.parted_ref, f32[2,8,1,256]{3,2,1,0:T(1,128)S(1)} %collective-permute-done.12.stats_ref, ...), custom_call_target="tpu_custom_call" | custom-call | flops 268435456 | bytes 1179648 | tf_op jit(solution)/shard_map/join/pallas_call | solution.py:190
  40.2 2.6 %close.1 = (bf16[256,1024]{1,0:T(8,128)(2,1)S(1)}, bf16[448,512]{1,0:T(8,128)(2,1)S(1)}, f32[8,1,256]{2,1,0:T(1,128)S(1)}, f32[8,1,256]{2,1,0:T(1,128)S(1)}, f32[8,128,256]{2,1,0:T(8,128)S(1)}) custom-call(s32[5]{0:T(128)S(1)} %stack.28.where_ref, ...), custom_call_target="tpu_custom_call", output_to_operand_aliasing={{2}: (3, {}), {3}: (4, {}), {4}: (5, {})} | custom-call | flops 536870912 | bytes 1310720 | tf_op jit(solution)/shard_map/close/pallas_call | solution.py:229
  42.8 1.5 %collective-permute-start.13 = (bf16[448,512]{1,0:T(8,128)(2,1)S(1)}, bf16[448,512]{1,0:T(8,128)(2,1)S(1)}, u32[]{:S(2)}, u32[]{:S(2)}) collective-permute-start(bf16[448,512]{1,0:T(8,128)(2,1)S(1)} %get-tuple-element.69), channel_id=1, source_target_pairs={{0,1},{1,0},{2,3},{3,2},{4,5},{5,4},{6,7},{7,6},{8,9},{9,8},{10,11... | collective-permute-start | bytes 1376264 | tf_op jit(solution)/shard_map/ppermute | solution.py:376
  44.3 1.6 %project_away.1 = (bf16[2,192,512]{2,1,0:T(8,128)(2,1)S(1)}, bf16[2,192,512]{2,1,0:T(8,128)(2,1)S(1)}) custom-call(s32[5]{0:T(128)S(1)} %stack.28.where_ref, bf16[256,1024]{1,0:T(8,128)(2,1)S(1)} %get-tuple-element.67.att_ref, bf16[1024,4096]{1,0:T(8,128)(2,1)S(1)} %bitcast.7), custom_call_target="tpu_custom_call" | custom-call | flops 301989888 | bytes 983040 | tf_op jit(solution)/shard_map/project_away/pallas_call | solution.py:252
  45.9 1.9 %collective-permute-start.17 = (bf16[2,192,512]{2,1,0:T(8,128)(2,1)S(1)}, bf16[2,192,512]{2,1,0:T(8,128)(2,1)S(1)}, u32[]{:S(2)}, u32[]{:S(2)}) collective-permute-start(bf16[2,192,512]{2,1,0:T(8,128)(2,1)S(1)} %get-tuple-element.75), channel_id=1, source_target_pairs={{0,2},{2,4},{4,6},{6,0},{1,3},{3,5},{5,7},{7,1},{8,10},{10,12},{12... | collective-permute-start | bytes 1179656 | tf_op jit(solution)/shard_map/ppermute | solution.py:377
  47.7 1.7 %collective-permute-start.18 = (bf16[2,192,512]{2,1,0:T(8,128)(2,1)S(1)}, bf16[2,192,512]{2,1,0:T(8,128)(2,1)S(1)}, u32[]{:S(2)}, u32[]{:S(2)}) collective-permute-start(bf16[2,192,512]{2,1,0:T(8,128)(2,1)S(1)} %get-tuple-element.76), channel_id=1, source_target_pairs={{0,6},{2,0},{4,2},{6,4},{1,7},{3,1},{5,3},{7,5},{8,14},{10,8},{12,... | collective-permute-start | bytes 1179656 | tf_op jit(solution)/shard_map/ppermute | solution.py:377
  49.4 1.9 %project_here.1 = (f32[2,192,512]{2,1,0:T(8,128)S(1)}, f32[448,512]{1,0:T(8,128)S(1)}) custom-call(s32[5]{0:T(128)S(1)} %stack.28.where_ref, bf16[256,1024]{1,0:T(8,128)(2,1)S(1)} %get-tuple-element.67.att_ref, bf16[1024,4096]{1,0:T(8,128)(2,1)S(1)} %bitcast.7), custom_call_target="tpu_custom_call" | custom-call | flops 301989888 | bytes 983040 | tf_op jit(solution)/shard_map/project_here/pallas_call | solution.py:275
  51.3 3.9 %collective-permute-done.13.got_ref = bf16[448,512]{1,0:T(8,128)(2,1)S(1)} collective-permute-done((bf16[448,512]{1,0:T(8,128)(2,1)S(1)}, bf16[448,512]{1,0:T(8,128)(2,1)S(1)}, u32[]{:S(2)}, u32[]{:S(2)}) %collective-permute-start.13) | collective-permute-done | bytes 458784 | tf_op jit(solution)/shard_map/ppermute | solution.py:376
  55.4 3.3 %collective-permute-start.16 = (bf16[256,512]{1,0:T(8,128)(2,1)S(1)}, bf16[256,512]{1,0:T(8,128)(2,1)S(1)}, u32[]{:S(2)}, u32[]{:S(2)}) collective-permute-start(bf16[256,512]{1,0:T(8,128)(2,1)S(1)} %get-tuple-element.73), channel_id=1, source_target_pairs={{0,4},{2,6},{4,0},{6,2},{1,5},{3,7},{5,1},{7,3},{8,12},{10,14},{12... | collective-permute-start | bytes 786440 | tf_op jit(solution)/shard_map/ppermute | solution.py:377
  58.8 1.5 %collective-permute-start.19 = (bf16[192,512]{1,0:T(8,128)(2,1)S(1)}, bf16[192,512]{1,0:T(8,128)(2,1)S(1)}, u32[]{:S(2)}, u32[]{:S(2)}) collective-permute-start(bf16[192,512]{1,0:T(8,128)(2,1)S(1)} %get-tuple-element.78), channel_id=1, source_target_pairs={{0,1},{1,0},{2,3},{3,2},{4,5},{5,4},{6,7},{7,6},{8,9},{9,8},{10,11... | collective-permute-start | bytes 589832 | tf_op jit(solution)/shard_map/ppermute | solution.py:376
  61.0 2.6 %collective-permute-start.15 = (bf16[64,512]{1,0:T(8,128)(2,1)S(1)}, bf16[64,512]{1,0:T(8,128)(2,1)S(1)}, u32[]{:S(2)}, u32[]{:S(2)}) collective-permute-start(bf16[64,512]{1,0:T(8,128)(2,1)S(1)} %get-tuple-element.72), channel_id=1, source_target_pairs={{0,6},{2,0},{4,2},{6,4},{1,7},{3,1},{5,3},{7,5},{8,14},{10,8},{12,... | collective-permute-start | bytes 196616 | tf_op jit(solution)/shard_map/ppermute | solution.py:377
  63.6 2.8 %collective-permute-done.14.refs_0_ = bf16[64,512]{1,0:T(8,128)(2,1)S(1)} collective-permute-done((bf16[64,512]{1,0:T(8,128)(2,1)S(1)}, bf16[64,512]{1,0:T(8,128)(2,1)S(1)}, u32[]{:S(2)}, u32[]{:S(2)}) %collective-permute-start.14) | collective-permute-done | bytes 65568 | tf_op jit(solution)/shard_map/ppermute | solution.py:377
  (37 shorter events, 5.1 us)
Async XLA Ops:
  0.0 11.3 %collective-permute-start.10 = (bf16[256,1024]{1,0:T(8,128)(2,1)}, bf16[256,1024]{1,0:T(8,128)(2,1)S(1)}, u32[]{:S(2)}, u32[]{:S(2)}) collective-permute-start(bf16[256,1024]{1,0:T(8,128)(2,1)} %queries_ref.1), channel_id=1, source_target_pairs={{0,8},{8,0},{1,9},{9,1},{2,10},{10,2},{3,11},{11,3},{4,12},{12,4},... | collective-permute-start | bytes 1572872 | tf_op jit(solution)/shard_map/ppermute | solution.py:352
  0.9 7.2 %collective-permute-start = (bf16[2,256,128]{2,1,0:T(8,128)(2,1)S(1)}, bf16[2,256,128]{2,1,0:T(8,128)(2,1)S(1)}, u32[]{:S(2)}, u32[]{:S(2)}) collective-permute-start(bf16[2,256,128]{2,1,0:T(8,128)(2,1)S(1)} %pad_maximum_fusion.own_ref), channel_id=1, source_target_pairs={{0,16},{16,32},{32,48},{48,64},{64,80},{80,96},{96,112},{112,0},{1... | collective-permute-start | bytes 393224 | tf_op jit(solution)/shard_map/ppermute | solution.py:359
  2.0 6.1 %collective-permute-start.6 = (bf16[2,256,128]{2,1,0:T(8,128)(2,1)S(1)}, bf16[2,256,128]{2,1,0:T(8,128)(2,1)S(1)}, u32[]{:S(2)}, u32[]{:S(2)}) collective-permute-start(bf16[2,256,128]{2,1,0:T(8,128)(2,1)S(1)} %pad_maximum_fusion.own_ref), channel_id=1, source_target_pairs={{0,112},{16,0},{32,16},{48,32},{64,48},{80,64},{96,80},{112,96},{1... | collective-permute-start | bytes 393224 | tf_op jit(solution)/shard_map/ppermute | solution.py:361
  8.1 9.7 %collective-permute-start.1 = (bf16[2,256,128]{2,1,0:T(8,128)(2,1)S(1)}, bf16[2,256,128]{2,1,0:T(8,128)(2,1)S(1)}, u32[]{:S(2)}, u32[]{:S(2)}) collective-permute-start(bf16[2,256,128]{2,1,0:T(8,128)(2,1)S(1)} %collective-permute-done.ahead_ref), channel_id=1, source_target_pairs={{0,16},{16,32},{32,48},{48,64},{64,80},{80,96},{96,112},{112,0},{1... | collective-permute-start | bytes 393224 | tf_op jit(solution)/shard_map/ppermute | solution.py:359
  8.1 9.7 %collective-permute-start.7 = (bf16[2,256,128]{2,1,0:T(8,128)(2,1)S(1)}, bf16[2,256,128]{2,1,0:T(8,128)(2,1)S(1)}, u32[]{:S(2)}, u32[]{:S(2)}) collective-permute-start(bf16[2,256,128]{2,1,0:T(8,128)(2,1)S(1)} %collective-permute-done.6.behind_ref), channel_id=1, source_target_pairs={{0,112},{16,0},{32,16},{48,32},{64,48},{80,64},{96,80},{112,96},{1... | collective-permute-start | bytes 393224 | tf_op jit(solution)/shard_map/ppermute | solution.py:361
  11.3 1.0 %copy-start = (bf16[256,1024]{1,0:T(8,128)(2,1)S(1)}, bf16[256,1024]{1,0:T(8,128)(2,1)}, u32[]{:S(2)}) copy-start(bf16[256,1024]{1,0:T(8,128)(2,1)} %queries_ref.1) | copy-start | bytes 1572868
  14.8 25.4 %slice-start = ((s8[8388608]{0:T(1024)(128)(4,1)}), s8[4194304]{0:T(1024)(128)(4,1)S(1)}, s32[]{:S(2)}) async-start(s8[8388608]{0:T(1024)(128)(4,1)} %bitcast.6), calls=%async_computation | async-start | bytes 8388608
  20.8 17.6 %collective-permute-start.11 = (bf16[8,128,256]{2,1,0:T(8,128)(2,1)S(1)}, bf16[8,128,256]{2,1,0:T(8,128)(2,1)S(1)}, u32[]{:S(2)}, u32[]{:S(2)}) collective-permute-start(bf16[8,128,256]{2,1,0:T(8,128)(2,1)S(1)} %get-tuple-element.59), channel_id=1, source_target_pairs={{0,8},{8,0},{1,9},{9,1},{2,10},{10,2},{3,11},{11,3},{4,12},{12,4},... | collective-permute-start | bytes 1572872 | tf_op jit(solution)/shard_map/ppermute | solution.py:352
  21.1 7.1 %collective-permute-start.2 = (bf16[2,256,128]{2,1,0:T(8,128)(2,1)S(1)}, bf16[2,256,128]{2,1,0:T(8,128)(2,1)S(1)}, u32[]{:S(2)}, u32[]{:S(2)}) collective-permute-start(bf16[2,256,128]{2,1,0:T(8,128)(2,1)S(1)} %collective-permute-done.1.ahead_ref), channel_id=1, source_target_pairs={{0,16},{16,32},{32,48},{48,64},{64,80},{80,96},{96,112},{112,0},{1... | collective-permute-start | bytes 393224 | tf_op jit(solution)/shard_map/ppermute | solution.py:359
  21.2 7.0 %collective-permute-start.8 = (bf16[2,256,128]{2,1,0:T(8,128)(2,1)S(1)}, bf16[2,256,128]{2,1,0:T(8,128)(2,1)S(1)}, u32[]{:S(2)}, u32[]{:S(2)}) collective-permute-start(bf16[2,256,128]{2,1,0:T(8,128)(2,1)S(1)} %collective-permute-done.7.behind_ref), channel_id=1, source_target_pairs={{0,112},{16,0},{32,16},{48,32},{64,48},{80,64},{96,80},{112,96},{1... | collective-permute-start | bytes 393224 | tf_op jit(solution)/shard_map/ppermute | solution.py:361
  28.2 6.2 %collective-permute-start.3 = (bf16[2,256,128]{2,1,0:T(8,128)(2,1)S(1)}, bf16[2,256,128]{2,1,0:T(8,128)(2,1)S(1)}, u32[]{:S(2)}, u32[]{:S(2)}) collective-permute-start(bf16[2,256,128]{2,1,0:T(8,128)(2,1)S(1)} %collective-permute-done.2.ahead_ref), channel_id=1, source_target_pairs={{0,16},{16,32},{32,48},{48,64},{64,80},{80,96},{96,112},{112,0},{1... | collective-permute-start | bytes 393224 | tf_op jit(solution)/shard_map/ppermute | solution.py:359
  28.2 8.4 %collective-permute-start.5 = (bf16[2,256,128]{2,1,0:T(8,128)(2,1)S(1)}, bf16[2,256,128]{2,1,0:T(8,128)(2,1)S(1)}, u32[]{:S(2)}, u32[]{:S(2)}) collective-permute-start(bf16[2,256,128]{2,1,0:T(8,128)(2,1)S(1)} %collective-permute-done.2.ahead_ref), channel_id=1, source_target_pairs={{0,8},{8,0},{1,9},{9,1},{2,10},{10,2},{3,11},{11,3},{4,12},{12,4},... | collective-permute-start | bytes 393224 | tf_op jit(solution)/shard_map/ppermute | solution.py:352
  28.2 8.4 %collective-permute-start.9 = (bf16[2,256,128]{2,1,0:T(8,128)(2,1)S(1)}, bf16[2,256,128]{2,1,0:T(8,128)(2,1)S(1)}, u32[]{:S(2)}, u32[]{:S(2)}) collective-permute-start(bf16[2,256,128]{2,1,0:T(8,128)(2,1)S(1)} %collective-permute-done.8.behind_ref), channel_id=1, source_target_pairs={{0,8},{8,0},{1,9},{9,1},{2,10},{10,2},{3,11},{11,3},{4,12},{12,4},... | collective-permute-start | bytes 393224 | tf_op jit(solution)/shard_map/ppermute | solution.py:352
  34.4 5.8 %collective-permute-start.4 = (bf16[2,256,128]{2,1,0:T(8,128)(2,1)S(1)}, bf16[2,256,128]{2,1,0:T(8,128)(2,1)S(1)}, u32[]{:S(2)}, u32[]{:S(2)}) collective-permute-start(bf16[2,256,128]{2,1,0:T(8,128)(2,1)S(1)} %collective-permute-done.3.ahead_ref), channel_id=1, source_target_pairs={{0,8},{8,0},{1,9},{9,1},{2,10},{10,2},{3,11},{11,3},{4,12},{12,4},... | collective-permute-start | bytes 393224 | tf_op jit(solution)/shard_map/ppermute | solution.py:352
  34.4 4.0 %collective-permute-start.12 = (f32[2,8,1,256]{3,2,1,0:T(1,128)S(1)}, f32[2,8,1,256]{3,2,1,0:T(1,128)S(1)}, u32[]{:S(2)}, u32[]{:S(2)}) collective-permute-start(f32[2,8,1,256]{3,2,1,0:T(1,128)S(1)} %get-tuple-element.60), channel_id=1, source_target_pairs={{0,8},{8,0},{1,9},{9,1},{2,10},{10,2},{3,11},{11,3},{4,12},{12,4},... | collective-permute-start | bytes 49160 | tf_op jit(solution)/shard_map/ppermute | solution.py:352
  34.9 5.3 %slice-start.1 = ((s8[8388608]{0:T(1024)(128)(4,1)}), s8[4194304]{0:T(1024)(128)(4,1)S(1)}, s32[]{:S(2)}) async-start(s8[8388608]{0:T(1024)(128)(4,1)} %bitcast.6), calls=%async_computation.1 | async-start | bytes 8388608
  42.8 12.5 %collective-permute-start.13 = (bf16[448,512]{1,0:T(8,128)(2,1)S(1)}, bf16[448,512]{1,0:T(8,128)(2,1)S(1)}, u32[]{:S(2)}, u32[]{:S(2)}) collective-permute-start(bf16[448,512]{1,0:T(8,128)(2,1)S(1)} %get-tuple-element.69), channel_id=1, source_target_pairs={{0,1},{1,0},{2,3},{3,2},{4,5},{5,4},{6,7},{7,6},{8,9},{9,8},{10,11... | collective-permute-start | bytes 1376264 | tf_op jit(solution)/shard_map/ppermute | solution.py:376
  45.9 12.8 %collective-permute-start.17 = (bf16[2,192,512]{2,1,0:T(8,128)(2,1)S(1)}, bf16[2,192,512]{2,1,0:T(8,128)(2,1)S(1)}, u32[]{:S(2)}, u32[]{:S(2)}) collective-permute-start(bf16[2,192,512]{2,1,0:T(8,128)(2,1)S(1)} %get-tuple-element.75), channel_id=1, source_target_pairs={{0,2},{2,4},{4,6},{6,0},{1,3},{3,5},{5,7},{7,1},{8,10},{10,12},{12... | collective-permute-start | bytes 1179656 | tf_op jit(solution)/shard_map/ppermute | solution.py:377
  47.7 10.9 %collective-permute-start.18 = (bf16[2,192,512]{2,1,0:T(8,128)(2,1)S(1)}, bf16[2,192,512]{2,1,0:T(8,128)(2,1)S(1)}, u32[]{:S(2)}, u32[]{:S(2)}) collective-permute-start(bf16[2,192,512]{2,1,0:T(8,128)(2,1)S(1)} %get-tuple-element.76), channel_id=1, source_target_pairs={{0,6},{2,0},{4,2},{6,4},{1,7},{3,1},{5,3},{7,5},{8,14},{10,8},{12,... | collective-permute-start | bytes 1179656 | tf_op jit(solution)/shard_map/ppermute | solution.py:377
  55.4 11.0 %collective-permute-start.16 = (bf16[256,512]{1,0:T(8,128)(2,1)S(1)}, bf16[256,512]{1,0:T(8,128)(2,1)S(1)}, u32[]{:S(2)}, u32[]{:S(2)}) collective-permute-start(bf16[256,512]{1,0:T(8,128)(2,1)S(1)} %get-tuple-element.73), channel_id=1, source_target_pairs={{0,4},{2,6},{4,0},{6,2},{1,5},{3,7},{5,1},{7,3},{8,12},{10,14},{12... | collective-permute-start | bytes 786440 | tf_op jit(solution)/shard_map/ppermute | solution.py:377
  58.8 7.6 %collective-permute-start.19 = (bf16[192,512]{1,0:T(8,128)(2,1)S(1)}, bf16[192,512]{1,0:T(8,128)(2,1)S(1)}, u32[]{:S(2)}, u32[]{:S(2)}) collective-permute-start(bf16[192,512]{1,0:T(8,128)(2,1)S(1)} %get-tuple-element.78), channel_id=1, source_target_pairs={{0,1},{1,0},{2,3},{3,2},{4,5},{5,4},{6,7},{7,6},{8,9},{9,8},{10,11... | collective-permute-start | bytes 589832 | tf_op jit(solution)/shard_map/ppermute | solution.py:376
  60.3 6.1 %collective-permute-start.14 = (bf16[64,512]{1,0:T(8,128)(2,1)S(1)}, bf16[64,512]{1,0:T(8,128)(2,1)S(1)}, u32[]{:S(2)}, u32[]{:S(2)}) collective-permute-start(bf16[64,512]{1,0:T(8,128)(2,1)S(1)} %get-tuple-element.71), channel_id=1, source_target_pairs={{0,2},{2,4},{4,6},{6,0},{1,3},{3,5},{5,7},{7,1},{8,10},{10,12},{12... | collective-permute-start | bytes 196616 | tf_op jit(solution)/shard_map/ppermute | solution.py:377
  61.0 5.4 %collective-permute-start.15 = (bf16[64,512]{1,0:T(8,128)(2,1)S(1)}, bf16[64,512]{1,0:T(8,128)(2,1)S(1)}, u32[]{:S(2)}, u32[]{:S(2)}) collective-permute-start(bf16[64,512]{1,0:T(8,128)(2,1)S(1)} %get-tuple-element.72), channel_id=1, source_target_pairs={{0,6},{2,0},{4,2},{6,4},{1,7},{3,1},{5,3},{7,5},{8,14},{10,8},{12,... | collective-permute-start | bytes 196616 | tf_op jit(solution)/shard_map/ppermute | solution.py:377
